TPU v7x, 256 devices: a 8x8x2 block of a 8x8x16 slice. The times are simulated.
256 devices in a mesh: grp: 2 (over z), bl: 128 (over x, y, core).
Axes of the slice: x: 8, y: 8, z: 2, core: 2. Of those that a mesh axis runs over, the one named last changes fastest.
The devices are a block of a 8x8x16 slice.
Arguments:
- vis: float32 [256, 512, 4, 128], P(('grp', 'bl')), parts along dimension 0, may hold values from -6 to 6
- sample_importance: float32 [256, 512], P(('grp', 'bl')), parts along dimension 0, may hold values from 0.1 to 1
- cells: int32 [256, 512, 64], P(('grp', 'bl')), parts along dimension 0, may hold values from 0 to 8191
- jones: float32 [512, 4, 128], replicated, may hold values from -3 to 3
- pairs: int32 [4, 512], P('grp'), parts along dimension 0, may hold values from 0 to 511
- pair_sequence: int32 [1024], P('grp'), parts along dimension 0, may hold values from 0 to 511, each once
Outputs:
- sky_grid: float32 [256, 4, 128], P(('grp', 'bl')), parts along dimension 0
- baseline_means: float32 [1024, 4, 128], P(('grp', 'bl')), parts along dimension 0
There are 2 independent parts, one for each index of `grp`. A program takes and returns all parts, laid end to end along the dimension named above; an argument that names none is the same for every part. Nothing has to cross between parts.
Inputs may be any that keep to these rules, and one draw needn't show every extreme that they name: `pair_sequence`: each baseline appears once.
All inputs are finite; a program needn't handle non-finite values.
Results may differ from a plain program's by a relative error of at most 0.005.
Values sent between devices are 32-bit elements; how exact they have to be, the bound alone decides.
A program may use at most 128 MiB of HBM per device.

v0:
```python
import math

import jax
import jax.numpy as jnp
from jax import lax
from jax.sharding import Mesh
from jax.sharding import PartitionSpec as P

GRID_V_CELLS = 64
ROWS_DEV = 1
BL = ("bl_0", "bl_1", "bl_2")
GRP_BL = ("grp", "bl_0", "bl_1", "bl_2")


def in_one_piece(arrays, axis, split_dim, concat_dim, along):
    widths = [math.prod(a.shape[along:]) for a in arrays]
    both = jnp.concatenate(
        [a.reshape(*a.shape[:along], w) for a, w in zip(arrays, widths)], axis=along
    )
    whole = lax.all_to_all(both, axis, split_axis=split_dim, concat_axis=concat_dim, tiled=True)
    tiles = jnp.split(whole, [sum(widths[:k]) for k in range(1, len(widths))], axis=along)
    return tuple((b.reshape(*whole.shape[:along], *a.shape[along:]) for a, b in zip(arrays, tiles)))


def cut_along(x, dim, length):
    before, after = (x.shape[:dim], x.shape[dim + 1 :])
    return jnp.moveaxis(x.reshape(*before, length, -1, *after), dim, 0)


def sum_at_owner(x, axis, dim):
    length = lax.axis_size(axis)
    tiles = lax.all_to_all(cut_along(x, dim, length), axis, 0, 0, tiled=True)
    return jnp.sum(tiles, axis=0)


def sum_by_axis(x, axes, dim):
    far, near = axes
    own = sum_at_owner(cut_along(x, dim, lax.axis_size(far)), near, dim + 1)
    return jnp.sum(lax.all_to_all(own, far, 0, 0, tiled=True), axis=0)


def select_part(source, index):
    half_width = source.shape[-1] // 2
    return (source[..., index, :half_width], source[..., index, half_width:])


def stokes_from(visibility, first_gain, second_gain):
    halfway = []
    for outer in range(2):
        for column in range(2):
            accum_real = 0.0
            accum_imag = 0.0
            for middle in range(2):
                gain_real, gain_imag = select_part(first_gain, 2 * outer + middle)
                data_real, data_imag = select_part(visibility, 2 * middle + column)
                accum_real = accum_real + gain_real * data_real - gain_imag * data_imag
                accum_imag = accum_imag + gain_real * data_imag + gain_imag * data_real
            halfway.append((accum_real, accum_imag))
    result = []
    for outer in range(2):
        for column in range(2):
            accum_real = 0.0
            accum_imag = 0.0
            for middle in range(2):
                left_real, left_imag = halfway[2 * outer + middle]
                gain_real, gain_imag = select_part(second_gain, 2 * column + middle)
                accum_real = accum_real + left_real * gain_real + left_imag * gain_imag
                accum_imag = accum_imag + left_imag * gain_real - left_real * gain_imag
            result.append((accum_real, accum_imag))
    stokes_real = [
        0.5 * (result[0][0] + result[3][0]),
        0.5 * (result[0][0] - result[3][0]),
        0.5 * (result[1][0] + result[2][0]),
        0.5 * (result[1][1] - result[2][1]),
    ]
    stokes_imag = [
        0.5 * (result[0][1] + result[3][1]),
        0.5 * (result[0][1] - result[3][1]),
        0.5 * (result[1][1] + result[2][1]),
        -0.5 * (result[1][0] - result[2][0]),
    ]
    return jnp.concatenate([jnp.stack(stokes_real, -2), jnp.stack(stokes_imag, -2)], -1)


def per_device(vis, sample_importance, cells, jones, pairs, pair_sequence):
    processor_array = lax.axis_size(BL)
    resident_epochs, station_pair_number = sample_importance.shape
    frequency_number = cells.shape[2]
    resident_station_pairs = station_pair_number // processor_array
    owned_slots = lax.dynamic_slice_in_dim(
        pair_sequence, lax.axis_index(BL) * resident_station_pairs, resident_station_pairs
    )
    vis_sorted = jnp.take(vis, pair_sequence, axis=1)
    weight_sorted = jnp.take(sample_importance, pair_sequence, axis=1)
    cell_sorted = jnp.take(cells, pair_sequence, axis=1)
    cell_float = cell_sorted.astype(jnp.float32)
    vis_local, weight_local, cell_arrived = in_one_piece(
        (vis_sorted, weight_sorted, cell_float), BL, 1, 0, 2
    )
    cell_local = cell_arrived.astype(jnp.int32)
    first_gain = jnp.take(jones, jnp.take(pairs[0], owned_slots), axis=0)[None]
    second_gain = jnp.take(jones, jnp.take(pairs[1], owned_slots), axis=0)[None]
    stokes = stokes_from(vis_local, first_gain, second_gain)
    weight_total = jnp.sum(weight_local, axis=0)
    means = jnp.sum(weight_local[:, :, None, None] * stokes, axis=0) / weight_total[:, None, None]
    leftover_rows = (weight_local[:, :, None, None] * (stokes - means[None])).astype(jnp.bfloat16)
    pair_count = leftover_rows.shape[0] * leftover_rows.shape[1]
    residual_rows = leftover_rows.reshape(pair_count, 8, frequency_number).transpose(0, 2, 1)
    grid_rows_total = ROWS_DEV * processor_array
    small_pairs = math.gcd(pair_count, 32)
    small_count = pair_count // small_pairs
    value_blocks = residual_rows.reshape(small_count, small_pairs * frequency_number, 8)
    index_blocks = cell_local.reshape(small_count, small_pairs * frequency_number)
    row_count = ROWS_DEV * lax.axis_size(BL)

    def add_rows(running, inputs):
        flat_values, flat_cells = inputs
        u_offset = flat_cells // GRID_V_CELLS
        u_onehot = (u_offset[:, None] == lax.iota(jnp.int32, row_count)).astype(jnp.bfloat16)
        v_onehot = (
            (flat_cells % GRID_V_CELLS)[:, None] == lax.iota(jnp.int32, GRID_V_CELLS)
        ).astype(jnp.bfloat16)
        placed = (u_onehot[:, :, None] * flat_values[:, None, :]).reshape(
            flat_values.shape[0], row_count * 8
        )
        added = lax.dot_general(
            placed, v_onehot, (((0,), (0,)), ((), ())), preferred_element_type=jnp.float32
        )
        return (running + added, None)

    start_rows = jnp.zeros((row_count * 8, GRID_V_CELLS), jnp.float32)
    final_rows, unused = lax.scan(add_rows, start_rows, (value_blocks, index_blocks))
    own_grid = sum_by_axis(
        final_rows.reshape(row_count, 8 * GRID_V_CELLS), (("bl_0", "bl_1"), "bl_2"), 0
    )
    scale_factor = math.sqrt(
        grid_rows_total
        * GRID_V_CELLS
        / (resident_epochs * processor_array * station_pair_number * frequency_number)
    )
    sky_grid = (own_grid * scale_factor).reshape(ROWS_DEV, 4, 2 * GRID_V_CELLS)
    return (sky_grid, means)


def solution(mesh):
    split = Mesh(mesh.devices.reshape(mesh.shape["grp"], 8, 8, 2), ("grp", "bl_0", "bl_1", "bl_2"))
    in_specs = (
        P(GRP_BL, None, None, None),
        P(GRP_BL, None),
        P(GRP_BL, None, None),
        P(),
        P("grp", None),
        P("grp"),
    )
    out_specs = (P(GRP_BL, None, None), P(GRP_BL, None, None))
    return jax.shard_map(
        per_device, mesh=split, in_specs=in_specs, out_specs=out_specs, check_vma=False
    )
```

profile of v0, /device:TPU:513, one launch (start us, length us, event | category | flops | bytes accessed | tf_op | source)
XLA Modules:
  0.0 157.9 jit_solution(17601390806596418162)
XLA Ops:
  1.5 3.5 %gather_fusion.1 = f32[512]{0:T(512)S(1)} fusion(f32[512]{0:T(512)S(1)} %bitcast.55, s32[1024]{0:T(1024)S(1)} %pad_clamp_fusion.3), kind=kCustom, calls=%fused_computation.5 | custom fusion | bytes 6144 | tf_op jit(solution)/shard_map/jit(_take)/gather | solution.py:94
  6.6 2.1 %gather_fusion = f32[512,4,128]{2,1,0:T(4,128)S(1)} fusion(f32[512,4,128]{2,1,0:T(4,128)S(1)} %bitcast.54, s32[1024]{0:T(1024)S(1)} %pad_clamp_fusion.3), kind=kCustom, calls=%fused_computation.4 | custom fusion | bytes 2099200 | tf_op jit(solution)/shard_map/jit(_take)/gather | solution.py:93
  8.7 1.8 %broadcast_select_fusion = f32[1,512,512]{2,0,1:T(1,128)S(1)} fusion(f32[1,512,512]{2,0,1:T(1,128)S(1)} %bitcast.59, pred[512]{0:T(512)(128)(4,1)S(1)} %get-tuple-element.123), kind=kLoop, calls=%fused_computation.28 | loop fusion | flops 262144 | bytes 2097664 | tf_op jit(solution)/shard_map/jit(_take)/select_n | solution.py:93
  10.5 2.5 %pad_maximum_fusion = f32[1,512,577]{2,0,1:T(1,128)} fusion(f32[1,512,64]{2,0,1:T(1,128)S(1)} %copy.28, f32[1,512,1]{2,0,1:T(1,128)S(1)} %copy.27, f32[1,512,512]{2,0,1:T(1,128)S(1)} %broadcast_select_fusion), kind=kLoop, calls=%fused_computation.29 | loop fusion | flops 590848 | bytes 2363392 | tf_op jit(solution)/shard_map/concatenate | solution.py:17
  13.0 27.6 %all-to-all-start = ((f32[1,512,577]{2,0,1:T(1,128)}), f32[1,512,577]{2,0,1:T(1,128)S(1)}, u32[]{:S(2)}, u32[]{:S(2)}) async-start(f32[1,512,577]{2,0,1:T(1,128)} %pad_maximum_fusion), calls=%async_computation | async-start | bytes 2621440 | tf_op jit(solution)/shard_map/all_to_all | solution.py:20
  42.2 1.8 %gather_fusion.4 = f32[4,4,128]{2,1,0:T(4,128)S(1)} fusion(f32[512,4,128]{2,1,0:T(4,128)} %param.15, s32[1024]{0:T(1024)S(1)} %pad_clamp_fusion.1), kind=kCustom, calls=%fused_computation.1.clone | custom fusion | bytes 16400 | tf_op jit(solution)/shard_map/jit(_take)/gather | solution.py:101
  44.0 1.8 %gather_fusion.6 = f32[4,4,128]{2,1,0:T(4,128)S(1)} fusion(f32[512,4,128]{2,1,0:T(4,128)} %param.15, s32[1024]{0:T(1024)S(1)} %pad_clamp_fusion), kind=kCustom, calls=%fused_computation.3.clone | custom fusion | bytes 16400 | tf_op jit(solution)/shard_map/jit(_take)/gather | solution.py:102
  46.0 30.6 %all-to-all-done = f32[1,512,577]{2,0,1:T(1,128)S(1)} async-done(((f32[1,512,577]{2,0,1:T(1,128)}), f32[1,512,577]{2,0,1:T(1,128)S(1)}, u32[]{:S(2)}, u32[]{:S(2)}) %all-to-all-start) | async-done | bytes 1181728 | tf_op jit(solution)/shard_map/all_to_all | solution.py:20
  76.6 4.6 %reduce.3 = f32[512,577]{1,0:T(8,128)} reduce(f32[1,512,577]{2,0,1:T(1,128)S(1)} %all-to-all-done, f32[]{:T(128)} %constant.149), dimensions={0}, to_apply=%all_to_all.15.reduce_sub_computation | reduce | bytes 2363396 | tf_op jit(solution)/shard_map/all_to_all | solution.py:20
  81.3 1.7 %all_to_all.16 = f32[128,4,577]{2,1,0:T(4,128)S(1)} reshape(f32[512,577]{1,0:T(8,128)} %reduce.3) | data formatting | bytes 2363392 | tf_op jit(solution)/shard_map/all_to_all | solution.py:20
  84.8 1.9 %reshape.225 = s32[16,2048]{1,0:T(8,128)} reshape(s32[128,4,64]{2,1,0:T(4,128)} %slice_convert_fusion) | data formatting | bytes 262144 | tf_op jit(solution)/shard_map/reshape | solution.py:113
  90.7 1.8 %sub.184 = f32[512,8,64]{2,1,0:T(8,128)S(1)} reshape(f32[128,4,4,128]{3,2,1,0:T(4,128)} %copy.31) | data formatting | bytes 2097152 | tf_op jit(solution)/shard_map/sub | solution.py:106
  92.6 1.5 fusion.12
  95.4 40.3 %while.13 = (s32[]{:T(128)}, f32[1024,64]{0,1:T(8,128)S(1)}, s32[16,2048]{1,0:T(8,128)}, bf16[16,2048,8]{1,2,0:T(8,128)(2,1)S(1)}, s32[]{:T(128)}, /*index=5*/s32[]{:T(128)}) while((s32[]{:T(128)}, f32[1024,64]{0,1:T(8,128)S(1)}, s32[16,2048]{1,0:T(8,128)}, bf16[16,2048,8]{1,2,0:T(8,128)(2,1)S(1)}, s32[]{:T(128)}, ...), condition=%wide.region_3.6_spmd.clone, body=%wide.region_2.5_spmd.clone.sunk | while | flops 271357952 | bytes 1728607 | solution.py:132
  96.4 1.5 fusion.22
  98.9 1.5 fusion.22
  101.4 1.5 fusion.22
  103.9 1.5 fusion.22
  106.4 1.5 fusion.22
  108.9 1.5 fusion.22
  111.4 1.5 fusion.22
  113.9 1.5 fusion.22
  116.4 1.5 fusion.22
  119.0 1.5 fusion.22
  121.5 1.5 fusion.22
  124.0 1.5 fusion.22
  126.5 1.5 fusion.22
  129.0 1.5 fusion.22
  131.5 1.5 fusion.22
  134.0 1.5 fusion.22
  136.2 4.4 %all_to_all.22 = f32[2,64,1,512]{3,1,2,0:T(8,128)S(1)} all-to-all(f32[2,64,1,512]{3,1,2,0:T(8,128)S(1)} %copy.35), channel_id=1, replica_groups=mesh['grp'=2,'bl_0'=8,'bl_1'=8,'bl_2'=2] {'bl_2'}, dimensions={0} | all-to-all | bytes 524288 | tf_op jit(solution)/shard_map/all_to_all | solution.py:32
  140.7 16.5 %all_to_all.23 = f32[64,1,512]{2,1,0:T(1,128)S(1)} all-to-all(f32[64,1,512]{2,1,0:T(1,128)S(1)} %reduce_sum.41), channel_id=1, replica_groups=mesh['grp'=2,'bl_0'=8,'bl_1'=8,'bl_2'=2] {'bl_0','bl_1'}, dimensions={0} | all-to-all | bytes 262144 | tf_op jit(solution)/shard_map/all_to_all | solution.py:39
  (127 shorter events, 28.1 us)
Async XLA Ops:
  0.6 6.0 %copy-start = (f32[1,512,4,128]{3,2,1,0:T(4,128)S(1)}, f32[1,512,4,128]{3,2,1,0:T(4,128)}, u32[]{:S(2)}) copy-start(f32[1,512,4,128]{3,2,1,0:T(4,128)} %param.12) | copy-start | bytes 3145732
  0.6 4.3 %copy-start.6 = (s32[512]{0:T(512)S(1)}, s32[512]{0:T(512)}, u32[]{:S(2)}) copy-start(s32[512]{0:T(512)} %param.17) | copy-start | bytes 6148
  0.7 0.8 copy-start.1
  0.7 4.5 %copy-start.4 = (s32[1,512,64]{1,2,0:T(8,128)S(1)}, s32[1,512,64]{1,2,0:T(8,128)}, u32[]{:S(2)}) copy-start(s32[1,512,64]{1,2,0:T(8,128)} %param.14) | copy-start | bytes 393220
  13.0 27.7 %copy-start.7 = (s32[2,512]{1,0:T(2,128)S(1)}, s32[2,512]{1,0:T(2,128)}, u32[]{:S(2)}) copy-start(s32[2,512]{1,0:T(2,128)} %param.16) | copy-start | bytes 12292
  13.0 63.6 %all-to-all-start = ((f32[1,512,577]{2,0,1:T(1,128)}), f32[1,512,577]{2,0,1:T(1,128)S(1)}, u32[]{:S(2)}, u32[]{:S(2)}) async-start(f32[1,512,577]{2,0,1:T(1,128)} %pad_maximum_fusion), calls=%async_computation | async-start | bytes 2621440 | tf_op jit(solution)/shard_map/all_to_all | solution.py:20
  84.8 2.4 %copy-start.2 = (f32[128,4,1]{2,1,0:T(4,128)S(1)}, f32[128,4,1]{2,1,0:T(4,128)}, u32[]{:S(2)}) copy-start(f32[128,4,1]{2,1,0:T(4,128)} %get-tuple-element.126) | copy-start | bytes 6148
  89.0 1.7 %copy-start.5 = (f32[4,4,128]{2,1,0:T(4,128)}, f32[4,4,128]{2,1,0:T(4,128)S(1)}, u32[]{:S(2)}) copy-start(f32[4,4,128]{2,1,0:T(4,128)S(1)} %broadcast_divide_fusion) | copy-start | bytes 24580
  94.3 1.1 copy-start.3
where the time goes:
time: 159 us; the launch traced here: 158 us
  local copies, waits for them, and re-layouts  35.3 us (22%)
  waiting for transfers between devices  30.6 us (19%)
  starting transfers between devices  27.6 us (17%)
  matrix products  23.7 us (15%)
  blocking collectives  20.9 us (13%)
  other arithmetic  17.9 us (11%)
    all_to_all x1, waiting for transfers between devices, in_one_piece(): lax.all_to_all(both, axis, split_axis=split_dim, concat_axis=concat_dim,...  30.6 us
    all_to_all x1, starting transfers between devices, in_one_piece(): lax.all_to_all(both, axis, split_axis=split_dim, concat_axis=concat_dim,...  27.6 us
    dot_general x16, matrix products, add_rows(): lax.dot_general(placed, v_onehot, (((0,), (0,)), ((), ())), preferred_ele...  23.7 us
    all_to_all x1, blocking collectives, sum_by_axis(): return jnp.sum(lax.all_to_all(own, far, 0, 0, tiled=True), axis=0)  16.5 us
    dynamic_slice x16, local copies, waits for them, and re-layouts, per_device(): lax.scan(add_rows, start_rows, (value_blocks, index_blocks))  13.6 us
    all_to_all x1, other arithmetic, in_one_piece(): lax.all_to_all(both, axis, split_axis=split_dim, concat_axis=concat_dim,...  4.64 us
    all_to_all x1, blocking collectives, sum_at_owner(): tiles = lax.all_to_all(cut_along(x, dim, length), axis, 0, 0, tiled=True)  4.37 us
    gather x1, local copies, waits for them, and re-layouts, per_device(): weight_sorted = jnp.take(sample_importance, pair_sequence, axis=1)  3.49 us
  transfers between devices with their start and end apart: 1, of which 1 were waited for; matrix products, arithmetic and copies ran while one was open for 3% of the time, Pallas kernels for 0%

commit v1 on v0

v1 whole, which is shorter than its diff:
```python
import functools
import math

import jax
import jax.numpy as jnp
from jax import lax
from jax.experimental import pallas as pl
from jax.experimental.pallas import tpu as pltpu
from jax.sharding import PartitionSpec as P

SUB, LANE = 8, 128
NT = (((1,), (1,)), ((), ()))

def half_pair(x0, x1, low):
    r0 = pltpu.roll(x0, 64, 1); r1 = pltpu.roll(x1, 64, 1)
    return jnp.where(low, x0, r1), jnp.where(low, r0, x1)

def interleave(x):
    row = lax.broadcasted_iota(jnp.int32, x.shape, 0)
    lane = lax.broadcasted_iota(jnp.int32, x.shape, 1)
    z = pltpu.roll(pltpu.roll(x, 4, 0), 64, 1)
    return jnp.where((row < 4) == (lane < 64), x, z)

def stage_gather(vis, jones, seq, pairs, w, cells_t, V, G, Q, CB, CR, WR, XU):
    nb = vis.shape[0] // 4
    for j in range(nb // 128):
        blk = cells_t[:, 128 * j:128 * (j + 1)]
        CB[128 * j:128 * (j + 1), :] = jnp.transpose(jnp.concatenate([blk, blk], 0))
    low = lax.broadcasted_iota(jnp.int32, (1, LANE), 1) < 64
    def body(r, _):
        half = nb // 4
        chip = lax.rem(r, half) // 2
        pair = 4 * chip + 2 * (r // half) + lax.rem(r, 2)
        b0 = seq[2 * pair]; b1 = seq[2 * pair + 1]
        for h, b in ((0, b0), (1, b1)):
            o = pl.multiple_of(8 * r + 4 * h, 4)
            V[pl.ds(o, 4), :] = vis[pl.ds(pl.multiple_of(4 * b, 4), 4), :]
            G[pl.ds(o, 4), :] = jones[pl.ds(pl.multiple_of(4 * pairs[0, b], 4), 4), :]
            Q[pl.ds(o, 4), :] = jones[pl.ds(pl.multiple_of(4 * pairs[1, b], 4), 4), :]
        cell = jnp.where(low, CB[pl.ds(b0, 1), :], CB[pl.ds(b1, 1), :])
        weight = jnp.where(low, w[b0], w[b1])
        CR[pl.ds(r, 1), :] = cell
        WR[pl.ds(r, 1), :] = weight
        row = 4 * (r // 2) + lax.rem(r, 2)
        XU[pl.ds(row, 1), :] = cell.astype(jnp.float32)
        XU[pl.ds(row + 2, 1), :] = weight
        return 0
    lax.fori_loop(0, nb // 2, body, 0, unroll=8)

def stage_stokes(V, G, Q, WR, VAL, place):
    ng = V.shape[0] // 64
    low = lax.broadcasted_iota(jnp.int32, (SUB, LANE), 1) < 64
    def body(g, _):
        def ld(ref, c):
            b = pl.multiple_of(64 * g, 64)
            return half_pair(ref[pl.ds(b + c, 8, stride=8), :], ref[pl.ds(b + 4 + c, 8, stride=8), :], low)
        v = [ld(V, c) for c in range(4)]
        gp = [ld(G, c) for c in range(4)]
        gq = [ld(Q, c) for c in range(4)]
        W = []
        for o in range(2):
            for c in range(2):
                ar = ai = 0.0
                for m in range(2):
                    gr, gi = gp[2 * o + m]; dr, di = v[2 * m + c]
                    ar = ar + gr * dr - gi * di
                    ai = ai + gr * di + gi * dr
                W.append((ar, ai))
        C = []
        for o in range(2):
            for c in range(2):
                ar = ai = 0.0
                for m in range(2):
                    lr, li = W[2 * o + m]; gr, gi = gq[2 * c + m]
                    ar = ar + lr * gr + li * gi
                    ai = ai + li * gr - lr * gi
                C.append((ar, ai))
        wh = 0.5 * WR[pl.ds(pl.multiple_of(8 * g, 8), 8), :]
        comps = [C[0][0] + C[3][0], C[0][0] - C[3][0], C[1][0] + C[2][0], C[1][1] - C[2][1],
                 C[0][1] + C[3][1], C[0][1] - C[3][1], C[1][1] + C[2][1], C[2][0] - C[1][0]]
        for j, x in enumerate(comps):
            place(VAL, g, j, wh * x)
        return 0
    lax.fori_loop(0, ng, body, 0)

def grid_rows(rows, val_of, cell_of, A, B, ACC, per):
    pos = lax.broadcasted_iota(jnp.int32, (16, LANE), 0).astype(jnp.float32).astype(jnp.bfloat16)
    def step(s, _):
        for q in range(per):
            r = s * per + q
            val = val_of(r)
            hi = val.astype(jnp.bfloat16)
            lo = (val - hi.astype(jnp.float32)).astype(jnp.bfloat16)
            both = jnp.concatenate([hi, lo], 0)
            cell = cell_of(r)
            top = cell >> 8
            bot = cell & 255
            topb = jnp.broadcast_to(top.astype(jnp.float32), (16, LANE)).astype(jnp.bfloat16)
            botb = jnp.broadcast_to(bot.astype(jnp.float32), (16, LANE)).astype(jnp.bfloat16)
            zero = jnp.zeros((16, LANE), jnp.bfloat16)
            one = jnp.ones((16, LANE), jnp.bfloat16)
            for i in range(32):
                A[16 * i:16 * i + 16, LANE * q:LANE * (q + 1)] = jnp.where(topb == jnp.bfloat16(i), both, zero)
            rel = botb - pos
            for n in range(16):
                B[16 * n:16 * n + 16, LANE * q:LANE * (q + 1)] = jnp.where(rel == jnp.bfloat16(16 * n), one, zero)
        ACC[...] += lax.dot_general(A[...], B[...], NT, preferred_element_type=jnp.float32)
        return 0
    lax.fori_loop(0, rows // per, step, 0)


MESH = pl.DeviceIdType.MESH
SMEM = pl.BlockSpec(memory_space=pltpu.SMEM)
VMEM = pl.BlockSpec(memory_space=pltpu.VMEM)
F32 = jnp.float32
BF16 = jnp.bfloat16
CELLS = 64
PER = 16
LIMIT = 60 * 1024 * 1024


def place(val, g, j, x):
    val[pl.ds(pl.multiple_of(64 * g, 64) + j, 8, stride=8), :] = x


def local_kernel(seq, pairs, w, vis, jones, cells_t, val, xu, acc, V, G, Q, CB, CR, WR, A, B):
    stage_gather(vis, jones, seq, pairs, w, cells_t, V, G, Q, CB, CR, WR, xu)
    stage_stokes(V, G, Q, WR, val, place)
    acc[...] = jnp.zeros_like(acc)
    grid_rows(
        CR.shape[0],
        lambda r: val[pl.ds(pl.multiple_of(8 * r, 8), 8), :],
        lambda r: CR[pl.ds(r, 1), :],
        A, B, acc, PER,
    )


def greet(n, me):
    barrier = pltpu.get_barrier_semaphore()

    def hello(k, _):
        pl.semaphore_signal(barrier, inc=1, device_id={"bl": lax.rem(me + k, n)}, device_id_type=MESH)
        return 0

    lax.fori_loop(1, n, hello, 0)
    pl.semaphore_wait(barrier, n - 1)


def remote(src, dst, send, recv, d):
    return pltpu.make_async_remote_copy(
        src_ref=src, dst_ref=dst, send_sem=send, recv_sem=recv, device_id={"bl": d}, device_id_type=MESH
    )


def sums_kernel(n, side, val, xu, out, xr, R1, SA, SB, RA, RB, TA, TB, UA, UB, send, recv):
    me = lax.axis_index("bl")
    core = lax.rem(me, 2)
    chip = me // 2
    x = chip // side
    y = lax.rem(chip, side)
    greet(n, me)

    first = remote(val.at[1 - core], R1, send.at[0], recv.at[0], 2 * chip + 1 - core)
    first.start()

    def deal(k, _):
        d = lax.rem(me + k, n)
        remote(xu.at[lax.rem(d, 2), d // 2], xr.at[me], send.at[1], recv.at[1], d).start()
        return 0

    lax.fori_loop(1, n, deal, 0)
    xr[me] = xu[core, chip]
    first.wait()

    def fold(i, _):
        a = i // side
        b = lax.rem(i, side)
        SA[a, b] = val[core, i, 0:8] + R1[i, 0:8]
        SB[b, a] = val[core, i, 8:16] + R1[i, 8:16]
        return 0

    lax.fori_loop(0, side * side, fold, 0, unroll=8)
    for k in range(1, side):
        xk = lax.rem(x + k, side)
        yk = lax.rem(y + k, side)
        remote(SA.at[xk], RA.at[k - 1], send.at[2], recv.at[2], (xk * side + y) * 2 + core).start()
        remote(SB.at[yk], RB.at[k - 1], send.at[3], recv.at[3], (x * side + yk) * 2 + core).start()
    remote(RA, RA, send.at[2], recv.at[2], me).wait_recv()
    remote(RB, RB, send.at[3], recv.at[3], me).wait_recv()
    for k in range(side):
        ta = SA[x, k]
        tb = SB[y, k]
        for m in range(side - 1):
            ta = ta + RA[m, k]
            tb = tb + RB[m, k]
        TA[k] = ta
        TB[k] = tb
    for k in range(1, side):
        xk = lax.rem(x + k, side)
        yk = lax.rem(y + k, side)
        remote(TA.at[yk], UA.at[k - 1], send.at[4], recv.at[4], (x * side + yk) * 2 + core).start()
        remote(TB.at[xk], UB.at[k - 1], send.at[5], recv.at[5], (xk * side + y) * 2 + core).start()
    remote(UA, UA, send.at[4], recv.at[4], me).wait_recv()
    remote(UB, UB, send.at[5], recv.at[5], me).wait_recv()
    out[0:8] = TA[y] + jnp.sum(UA[...], axis=0)
    out[8:16] = TB[x] + jnp.sum(UB[...], axis=0)
    remote(xr.at[1:n], xr.at[1:n], send.at[1], recv.at[1], me).wait_recv()
    remote(xr.at[1:n], xr.at[1:n], send.at[1], recv.at[1], me).wait_send()
    remote(RA, RA, send.at[2], recv.at[2], me).wait_send()
    remote(RB, RB, send.at[3], recv.at[3], me).wait_send()
    remote(UA, UA, send.at[4], recv.at[4], me).wait_send()
    remote(UB, UB, send.at[5], recv.at[5], me).wait_send()


def mean_kernel(n, scale, sums, xr, acc_in, grid, means, acc, MN, XC, XW, A, B):
    acc[...] = acc_in[...]
    for j in range(2):
        XC[j] = xr[:, j, :].astype(jnp.int32)
        XW[j] = xr[:, 2 + j, :]
        m = sums[8 * j:8 * j + 8, :] / jnp.sum(XW[j], axis=0, keepdims=True)
        MN[j] = -m
        y = interleave(m)
        means[2 * j] = y[0:4]
        means[2 * j + 1] = y[4:8]
    for j in range(2):
        grid_rows(
            n,
            lambda t: MN[j] * XW[j, pl.ds(t, 1), :],
            lambda t: XC[j, pl.ds(t, 1), :],
            A, B, acc, PER,
        )

    for i in range(32):
        for h in range(2):
            s = slice(128 * h, 128 * h + 128)
            y = interleave(acc[16 * i:16 * i + 8, s] + acc[16 * i + 8:16 * i + 16, s]) * scale
            grid[4 * i + 2 * h] = y[0:4]
            grid[4 * i + 2 * h + 1] = y[4:8]


def gather_kernel(n, grid, out, buf, send, recv):
    me = lax.axis_index("bl")
    greet(n, me)

    def deal(k, _):
        d = lax.rem(me + k, n)
        remote(grid.at[d], buf.at[me], send, recv, d).start()
        return 0

    lax.fori_loop(1, n, deal, 0)
    buf[me] = grid[me]
    remote(buf.at[1:n], buf.at[1:n], send, recv, me).wait_recv()
    out[0] = jnp.sum(buf[...], axis=0)
    remote(buf.at[1:n], buf.at[1:n], send, recv, me).wait_send()


def per_device(n, vis, weight, cells, jones, pairs, seq):
    side = math.isqrt(n // 2)
    nb = weight.shape[1]
    rows = nb // 2
    chans = cells.shape[2]
    sds = jax.ShapeDtypeStruct
    vm = pltpu.VMEM
    val, xu, acc = pl.pallas_call(
        local_kernel,
        out_shape=(sds((4 * nb, 128), F32), sds((4 * n, 128), F32), sds((512, 256), F32)),
        in_specs=[SMEM, SMEM, SMEM, VMEM, VMEM, VMEM],
        out_specs=(VMEM, VMEM, VMEM),
        scratch_shapes=[vm((4 * nb, 128), F32)] * 3
        + [
            vm((nb, 128), jnp.int32),
            vm((rows, 128), jnp.int32),
            vm((rows, 128), F32),
            vm((512, 128 * PER), BF16),
            vm((256, 128 * PER), BF16),
        ],
        compiler_params=pltpu.CompilerParams(vmem_limit_bytes=LIMIT),
    )(seq, pairs, weight[0], vis.reshape(4 * nb, 128), jones.reshape(-1, 128), jnp.swapaxes(cells[0], 0, 1))
    sq = side * side
    sums, xr = pl.pallas_call(
        functools.partial(sums_kernel, n, side),
        out_shape=(sds((16, 128), F32), sds((n, 4, 128), F32)),
        in_specs=[VMEM, VMEM],
        out_specs=(VMEM, VMEM),
        scratch_shapes=[
            vm((sq, 16, 128), F32),
            vm((side, side, 8, 128), F32),
            vm((side, side, 8, 128), F32),
            vm((side - 1, side, 8, 128), F32),
            vm((side - 1, side, 8, 128), F32),
            vm((side, 8, 128), F32),
            vm((side, 8, 128), F32),
            vm((side - 1, 8, 128), F32),
            vm((side - 1, 8, 128), F32),
            pltpu.SemaphoreType.DMA((6,)),
            pltpu.SemaphoreType.DMA((6,)),
        ],
        compiler_params=pltpu.CompilerParams(collective_id=0, has_side_effects=True),
    )(val.reshape(2, sq, 16, 128), xu.reshape(2, sq, 4, 128))
    scale = math.sqrt(n * CELLS / (n * nb * chans))
    grid, means = pl.pallas_call(
        functools.partial(mean_kernel, n, scale),
        out_shape=(sds((n, 4, 128), F32), sds((4, 4, 128), F32)),
        in_specs=[VMEM, VMEM, VMEM],
        out_specs=(VMEM, VMEM),
        scratch_shapes=[
            vm((512, 256), F32),
            vm((2, 8, 128), F32),
            vm((2, n, 128), jnp.int32),
            vm((2, n, 128), F32),
            vm((512, 128 * PER), BF16),
            vm((256, 128 * PER), BF16),
        ],
        compiler_params=pltpu.CompilerParams(vmem_limit_bytes=LIMIT),
    )(sums, xr, acc)
    sky = pl.pallas_call(
        functools.partial(gather_kernel, n),
        out_shape=sds((1, 4, 128), F32),
        in_specs=[VMEM],
        out_specs=VMEM,
        scratch_shapes=[vm((n, 4, 128), F32), pltpu.SemaphoreType.DMA, pltpu.SemaphoreType.DMA],
        compiler_params=pltpu.CompilerParams(collective_id=1, has_side_effects=True),
    )(grid)
    return sky, means


def solution(mesh):
    both = ("grp", "bl")
    return jax.shard_map(
        functools.partial(per_device, mesh.shape["bl"]),
        mesh=mesh,
        in_specs=(P(both, None, None, None), P(both, None), P(both, None, None), P(), P("grp", None), P("grp")),
        out_specs=(P(both, None, None), P(both, None, None)),
        check_vma=False,
    )
```

time: 159 us -> 115 us (0.72)
  Pallas kernels: 0 us -> 113 us
  local copies, waits for them, and re-layouts: 35.3 us -> 1.26 us
  waiting for transfers between devices: 30.6 us -> 0 us
  starting transfers between devices: 27.6 us -> 0 us
  matrix products: 23.7 us -> 0 us
  blocking collectives: 20.9 us -> 0 us
  other arithmetic: 17.9 us -> 0 us
    pallas_call x0 -> x4, Pallas kernels: none -> 113 us  [the longest x1 48.2 us: per_device(): pl.pallas_call(functools.partial(sums_kernel, n, side), out_shape=(sds((1...]
    all_to_all x1 -> x0, waiting for transfers between devices: 30.6 us -> none  [in_one_piece(): lax.all_to_all(both, axis, split_axis=split_dim, concat_axis=concat_dim,...]
    all_to_all x1 -> x0, starting transfers between devices: 27.6 us -> none  [in_one_piece(): lax.all_to_all(both, axis, split_axis=split_dim, concat_axis=concat_dim,...]
    dot_general x16 -> x0, matrix products: 23.7 us -> none  [add_rows(): lax.dot_general(placed, v_onehot, (((0,), (0,)), ((), ())), preferred_ele...]
    all_to_all x2 -> x0, blocking collectives: 20.9 us -> none  [the longest x1 16.5 us: sum_by_axis(): return jnp.sum(lax.all_to_all(own, far, 0, 0, tiled=True), axis=0)]
    dynamic_slice x16 -> x0, local copies, waits for them, and re-layouts: 13.6 us -> none  [per_device(): lax.scan(add_rows, start_rows, (value_blocks, index_blocks))]
    gather x8 -> x0, local copies, waits for them, and re-layouts: 11.6 us -> none  [the longest x1 3.49 us: per_device(): weight_sorted = jnp.take(sample_importance, pair_sequence, axis=1)]
    all_to_all x1 -> x0, other arithmetic: 4.64 us -> none  [in_one_piece(): lax.all_to_all(both, axis, split_axis=split_dim, concat_axis=concat_dim,...]
  transfers between devices with their start and end apart: 1 -> 0, of which waited for: 1 -> 0; matrix products, arithmetic and copies ran while one was open for 3% -> 0% of each run, Pallas kernels for 0% -> 0%
where the time goes in v1:
time: 115 us
  Pallas kernels  113 us (98%)
  local copies, waits for them, and re-layouts  1.26 us (1%)
    pallas_call x1, Pallas kernels, per_device(): pl.pallas_call(functools.partial(sums_kernel, n, side), out_shape=(sds((1...  48.2 us
    pallas_call x1, Pallas kernels, per_device(): pl.pallas_call(local_kernel, out_shape=(sds((4 * nb, 128), F32), sds((4 *...  26.9 us
    pallas_call x1, Pallas kernels, per_device(): pl.pallas_call(functools.partial(gather_kernel, n), out_shape=sds((1, 4,...  20.9 us
    pallas_call x1, Pallas kernels, per_device(): pl.pallas_call(functools.partial(mean_kernel, n, scale), out_shape=(sds((...  17.3 us

profile of v1, /device:TPU:513, one launch (start us, length us, event | category | flops | bytes accessed | tf_op | source)
XLA Modules:
  0.0 115.2 jit_solution(2334488575690176556)
XLA Ops:
  0.6 26.9 %shard_map.77 = (f32[2048,128]{1,0:T(8,128)}, f32[512,128]{1,0:T(8,128)}, f32[512,256]{1,0:T(8,128)}) custom-call(s32[512]{0:T(512)} %seq.1, s32[2,512]{1,0:T(2,128)} %pairs.1, f32[512]{0:T(512)} %bitcast.13, f32[2048,128]{1,0:T(8,128)} %bitcast.9, f32[2048,128]{1,0:T(8,128)} %bitcast.10, s32[64,512]{1,0:T(8,128)} %bitcast.12), custom_call_target="tpu_custom_call" | custom-call | tf_op jit(solution)/shard_map/pallas_call | solution.py:264
  27.5 48.2 %shard_map.78 = (f32[16,128]{1,0:T(8,128)}, f32[128,4,128]{2,1,0:T(4,128)}) custom-call(f32[2,64,16,128]{3,2,1,0:T(8,128)} %bitcast.8, f32[2,64,4,128]{3,2,1,0:T(4,128)} %bitcast.11), custom_call_target="tpu_custom_call" | custom-call | tf_op jit(solution)/shard_map/pallas_call | solution.py:280
  75.7 17.3 %shard_map.79 = (f32[128,4,128]{2,1,0:T(4,128)}, f32[4,4,128]{2,1,0:T(4,128)}) custom-call(f32[16,128]{1,0:T(8,128)} %get-tuple-element.11.sums, f32[128,4,128]{2,1,0:T(4,128)} %get-tuple-element.12.xr, f32[512,256]{1,0:T(8,128)} %get-tuple-element.13.acc_in), custom_call_target="tpu_custom_call" | custom-call | tf_op jit(solution)/shard_map/pallas_call | solution.py:301
  93.0 20.9 %shard_map.80 = f32[1,4,128]{2,1,0:T(4,128)} custom-call(f32[128,4,128]{2,1,0:T(4,128)} %get-tuple-element.14.grid), custom_call_target="tpu_custom_call" | custom-call | tf_op jit(solution)/shard_map/pallas_call | solution.py:316
  113.9 1.3 %copy.9 = f32[1,4,128]{2,1,0:T(4,128)} copy(f32[1,4,128]{2,1,0:T(4,128)} %shard_map.80) | data formatting | bytes 4096

commit v2 on v0

v2 whole, which is shorter than its diff:
```python
import functools
import math

import jax
import jax.numpy as jnp
from jax import lax
from jax.experimental import pallas as pl
from jax.experimental.pallas import tpu as pltpu
from jax.sharding import PartitionSpec as P

MESH = pl.DeviceIdType.MESH
SMEM = pl.BlockSpec(memory_space=pltpu.SMEM)
VMEM = pl.BlockSpec(memory_space=pltpu.VMEM)
F32 = jnp.float32
BF16 = jnp.bfloat16
I32 = jnp.int32
V_CELLS = 64
LANE = 128
TOPS = 32
BOTS = 256
PER = 16
LIMIT = 60 * 1024 * 1024
NT = (((1,), (1,)), ((), ()))


def half_pair(x0, x1, low):
    r0 = pltpu.roll(x0, 64, 1)
    r1 = pltpu.roll(x1, 64, 1)
    return jnp.where(low, x0, r1), jnp.where(low, r0, x1)


def interleave(x):
    row = lax.broadcasted_iota(I32, x.shape, 0)
    lane = lax.broadcasted_iota(I32, x.shape, 1)
    z = pltpu.roll(pltpu.roll(x, 4, 0), 64, 1)
    return jnp.where((row < 4) == (lane < 64), x, z)


def slot_pair(r, nb):
    half = nb // 4
    core, chip, j = r // half, lax.rem(r, half) // 2, lax.rem(r, 2)
    return core, chip, j, 4 * chip + 2 * core + j


def stage_cells(side, seq, w, cells_t, CB, CR, WR, XU):
    nb = seq.shape[0]
    for j in range(nb // LANE):
        blk = cells_t[:, LANE * j:LANE * (j + 1)]
        CB[LANE * j:LANE * (j + 1), :] = jnp.transpose(jnp.concatenate([blk, blk], 0))
    low = lax.broadcasted_iota(I32, (1, LANE), 1) < 64

    def body(r, _):
        core, chip, j, pair = slot_pair(r, nb)
        b0 = seq[2 * pair]
        b1 = seq[2 * pair + 1]
        cell = jnp.where(low, CB[pl.ds(b0, 1), :], CB[pl.ds(b1, 1), :])
        weight = jnp.where(low, w[b0], w[b1])
        CR[pl.ds(r, 1), :] = cell
        WR[pl.ds(r, 1), :] = weight
        XU[core, j, chip // side, lax.rem(chip, side)] = jnp.concatenate([cell.astype(F32), weight], 0)
        return 0

    lax.fori_loop(0, nb // 2, body, 0, unroll=8)


def stage_rows(seq, pairs, vis, jones, V, G, Q):
    nb = seq.shape[0]

    def body(r, _):
        pair = slot_pair(r, nb)[3]
        for h in range(2):
            b = seq[2 * pair + h]
            o = pl.multiple_of(8 * r + 4 * h, 4)
            V[pl.ds(o, 4), :] = vis[pl.ds(pl.multiple_of(4 * b, 4), 4), :]
            G[pl.ds(o, 4), :] = jones[pl.ds(pl.multiple_of(4 * pairs[0, b], 4), 4), :]
            Q[pl.ds(o, 4), :] = jones[pl.ds(pl.multiple_of(4 * pairs[1, b], 4), 4), :]
        return 0

    lax.fori_loop(0, nb // 2, body, 0, unroll=8)


def stage_stokes(V, G, Q, WR, VAL):
    low = lax.broadcasted_iota(I32, (8, LANE), 1) < 64

    def body(g, _):
        base = pl.multiple_of(64 * g, 64)

        def ld(ref, c):
            return half_pair(ref[pl.ds(base + c, 8, stride=8), :], ref[pl.ds(base + 4 + c, 8, stride=8), :], low)

        v = [ld(V, c) for c in range(4)]
        gp = [ld(G, c) for c in range(4)]
        gq = [ld(Q, c) for c in range(4)]
        W = []
        for o in range(2):
            for c in range(2):
                ar = ai = 0.0
                for m in range(2):
                    gr, gi = gp[2 * o + m]
                    dr, di = v[2 * m + c]
                    ar = ar + gr * dr - gi * di
                    ai = ai + gr * di + gi * dr
                W.append((ar, ai))
        C = []
        for o in range(2):
            for c in range(2):
                ar = ai = 0.0
                for m in range(2):
                    lr, li = W[2 * o + m]
                    gr, gi = gq[2 * c + m]
                    ar = ar + lr * gr + li * gi
                    ai = ai + li * gr - lr * gi
                C.append((ar, ai))
        wh = 0.5 * WR[pl.ds(pl.multiple_of(8 * g, 8), 8), :]
        comps = [
            C[0][0] + C[3][0],
            C[0][0] - C[3][0],
            C[1][0] + C[2][0],
            C[1][1] - C[2][1],
            C[0][1] + C[3][1],
            C[0][1] - C[3][1],
            C[1][1] + C[2][1],
            C[2][0] - C[1][0],
        ]
        for j, x in enumerate(comps):
            VAL[pl.ds(base + j, 8, stride=8), :] = wh * x
        return 0

    lax.fori_loop(0, VAL.shape[0] // 64, body, 0)


def build(first, val_of, cell_of, A, B):
    pos = lax.broadcasted_iota(I32, (16, LANE), 0).astype(F32).astype(BF16)
    zero = jnp.zeros((16, LANE), BF16)
    one = jnp.ones((16, LANE), BF16)
    for q in range(PER):
        s = slice(LANE * q, LANE * (q + 1))
        val = val_of(first + q)
        hi = val.astype(BF16)
        lo = (val - hi.astype(F32)).astype(BF16)
        both = jnp.concatenate([hi, lo], 0)
        cell = cell_of(first + q)
        top = jnp.broadcast_to((cell >> 8).astype(F32), (16, LANE)).astype(BF16)
        rel = jnp.broadcast_to((cell & 255).astype(F32), (16, LANE)).astype(BF16) - pos
        for i in range(TOPS):
            A[16 * i:16 * i + 16, s] = jnp.where(top == BF16(i), both, zero)
        for i in range(BOTS // 16):
            B[16 * i:16 * i + 16, s] = jnp.where(rel == BF16(16 * i), one, zero)


def add_rows(first, rows, val_of, cell_of, A, B, ACC):
    def dot(p):
        ACC[...] += lax.dot_general(A[p][...], B[p][...], NT, preferred_element_type=F32)

    def step(s, _):
        base = first + 2 * PER * s
        build(base + PER, val_of, cell_of, A[1], B[1])
        dot(0)
        build(base + 2 * PER, val_of, cell_of, A[0], B[0])
        dot(1)
        return 0

    lax.fori_loop(0, rows // (2 * PER), step, 0)


def remote(src, dst, send, recv, i, d):
    return pltpu.make_async_remote_copy(
        src_ref=src,
        dst_ref=dst,
        send_sem=send.at[i],
        recv_sem=recv.at[i],
        device_id={"bl": d},
        device_id_type=MESH,
    )


def local_kernel(side, seq, pairs, w, vis, jones, cells_t, VAL, CR, XU, V, G, Q, CB, WR):
    stage_cells(side, seq, w, cells_t, CB, CR, WR, XU)
    stage_rows(seq, pairs, vis, jones, V, G, Q)
    stage_stokes(V, G, Q, WR, VAL)


def whole_kernel(n, side, scale, VAL, CR, XU, sky, means,
                 PX, XA, XB, YA, YB, R1, SA, SB, RA, RB, TA, TB, UA, UB,
                 ACC, MN, A0, B0, A1, B1, GR, PG, GA, GB, HA, HB, KA, KB, LA, LB, send, recv):
    me = lax.axis_index("bl")
    core = lax.rem(me, 2)
    chip = me // 2
    x = chip // side
    y = lax.rem(chip, side)
    mate = 2 * chip + 1 - core
    half = 8 * side * side * 2
    ring = [(lax.rem(x + k, side), lax.rem(y + k, side)) for k in range(1, side)]

    def at_x(xk):
        return (xk * side + y) * 2 + core

    def at_y(yk):
        return (x * side + yk) * 2 + core

    def landed(ref, i):
        remote(ref, ref, send, recv, i, mate).wait_recv()

    def sent(ref, i):
        remote(ref, ref, send, recv, i, mate).wait_send()

    barrier = pltpu.get_barrier_semaphore()
    for xk, yk in ring:
        pl.semaphore_signal(barrier, inc=1, device_id={"bl": at_x(xk)}, device_id_type=MESH)
        pl.semaphore_signal(barrier, inc=1, device_id={"bl": at_y(yk)}, device_id_type=MESH)
    pl.semaphore_signal(barrier, inc=1, device_id={"bl": mate}, device_id_type=MESH)

    pl.semaphore_wait(barrier, 2 * side - 1)
    remote(VAL.at[pl.ds(pl.multiple_of((1 - core) * half, half), half)], R1, send, recv, 5, mate).start()
    remote(XU.at[1 - core], PX, send, recv, 0, mate).start()

    rows = CR.shape[0]

    def own_val(r):
        return VAL[pl.ds(pl.multiple_of(8 * lax.rem(r, rows), 8), 8), :]

    def own_cell(r):
        return CR[pl.ds(lax.rem(r, rows), 1), :]

    bufs = (A0, A1), (B0, B1)
    ACC[...] = jnp.zeros_like(ACC)
    build(0, own_val, own_cell, A0, B0)
    landed(R1, 5)

    def fold(i, _):
        a = i // side
        b = lax.rem(i, side)
        mine = pl.multiple_of(core * half + 16 * i, 16)
        other = pl.multiple_of(16 * i, 16)
        SA[a, b] = VAL[pl.ds(mine, 8), :] + R1[pl.ds(other, 8), :]
        SB[b, a] = VAL[pl.ds(mine + 8, 8), :] + R1[pl.ds(other + 8, 8), :]
        return 0

    lax.fori_loop(0, side * side, fold, 0, unroll=8)
    for k, (xk, yk) in enumerate(ring):
        remote(SA.at[xk], RA.at[k], send, recv, 6, at_x(xk)).start()
        remote(SB.at[yk], RB.at[k], send, recv, 7, at_y(yk)).start()
    landed(PX, 0)
    for k, (xk, yk) in enumerate(ring, 1):
        remote(XU.at[core, 0, xk], XA.at[0, k], send, recv, 1, at_x(xk)).start()
        remote(PX.at[0, xk], XA.at[1, k], send, recv, 1, at_x(xk)).start()
        remote(XU.at[core, 1, :, yk], XB.at[0, k], send, recv, 2, at_y(yk)).start()
        remote(PX.at[1, :, yk], XB.at[1, k], send, recv, 2, at_y(yk)).start()
    XA[0, 0] = XU[core, 0, x]
    XA[1, 0] = PX[0, x]
    XB[0, 0] = XU[core, 1, :, y]
    XB[1, 0] = PX[1, :, y]
    add_rows(0, 5 * rows // 8, own_val, own_cell, *bufs, ACC)
    landed(RA, 6)
    landed(RB, 7)
    for k in range(side):
        ta = SA[x, k]
        tb = SB[y, k]
        for m in range(side - 1):
            ta = ta + RA[m, k]
            tb = tb + RB[m, k]
        TA[k] = ta
        TB[k] = tb
    for k, (xk, yk) in enumerate(ring):
        remote(TA.at[yk], UA.at[k], send, recv, 8, at_y(yk)).start()
        remote(TB.at[xk], UB.at[k], send, recv, 9, at_x(xk)).start()
    landed(XA.at[:, 1:side], 1)
    landed(XB.at[:, 1:side], 2)
    for k, (xk, yk) in enumerate(ring, 1):
        remote(XA.at[:, :, yk], YA.at[k], send, recv, 3, at_y(yk)).start()
        remote(XB.at[:, :, xk], YB.at[k], send, recv, 4, at_x(xk)).start()
    YA[0] = XA[:, :, y]
    YB[0] = XB[:, :, x]
    add_rows(5 * rows // 8, 3 * rows // 8, own_val, own_cell, *bufs, ACC)
    landed(YA.at[1:side], 3)
    landed(YB.at[1:side], 4)
    landed(UA, 8)
    landed(UB, 9)

    for j, (t, u, at, Y) in enumerate(((TA, UA, y, YA), (TB, UB, x, YB))):
        total = t[at] + jnp.sum(u[...], axis=0)
        m = total / jnp.sum(Y[:, :, :, 1, :].reshape(n, LANE), axis=0, keepdims=True)
        MN[j] = -m
        z = interleave(m)
        means[2 * j] = z[0:4]
        means[2 * j + 1] = z[4:8]
    for j, Y in enumerate((YA, YB)):
        def sample(t, row, Y=Y):
            t = lax.rem(t, n)
            return Y[t // (2 * side), lax.rem(t, 2 * side) // side, lax.rem(t, side), pl.ds(row, 1), :]

        def mean_val(t, j=j, sample=sample):
            return MN[j] * sample(t, 1)

        def mean_cell(t, sample=sample):
            return sample(t, 0).astype(I32)

        build(0, mean_val, mean_cell, A0, B0)
        add_rows(0, n, mean_val, mean_cell, *bufs, ACC)

    for i in range(TOPS):
        for h in range(BOTS // LANE):
            s = slice(LANE * h, LANE * (h + 1))
            z = interleave(ACC[16 * i:16 * i + 8, s] + ACC[16 * i + 8:16 * i + 16, s]) * scale
            for e in range(2):
                d = 4 * i + 2 * h + e
                GR[d % 2, d // 2 // side, d // 2 % side] = z[4 * e:4 * e + 4]

    remote(GR.at[1 - core], PG, send, recv, 10, mate).start()
    landed(PG, 10)
    for a in range(side):
        z = GR[core, a] + PG[a]
        GA[a] = z[:, 0:2]
        for b in range(side):
            GB[b, a] = z[b, 2:4]
    for k, (xk, yk) in enumerate(ring):
        remote(GA.at[xk], HA.at[k], send, recv, 11, at_x(xk)).start()
        remote(GB.at[yk], HB.at[k], send, recv, 12, at_y(yk)).start()
    landed(HA, 11)
    landed(HB, 12)
    KA[...] = GA[x] + jnp.sum(HA[...], axis=0)
    KB[...] = GB[y] + jnp.sum(HB[...], axis=0)
    for k, (xk, yk) in enumerate(ring):
        remote(KA.at[yk], LA.at[k], send, recv, 13, at_y(yk)).start()
        remote(KB.at[xk], LB.at[k], send, recv, 14, at_x(xk)).start()
    landed(LA, 13)
    landed(LB, 14)
    sky[0, 0:2] = KA[y] + jnp.sum(LA[...], axis=0)
    sky[0, 2:4] = KB[x] + jnp.sum(LB[...], axis=0)
    for ref, i in (
        (PX, 0), (XA.at[:, 1:side], 1), (XB.at[:, 1:side], 2), (YA.at[1:side], 3), (YB.at[1:side], 4), (R1, 5),
        (RA, 6), (RB, 7), (UA, 8), (UB, 9), (PG, 10), (HA, 11), (HB, 12), (LA, 13), (LB, 14),
    ):
        sent(ref, i)


def per_device(n, vis, weight, cells, jones, pairs, seq):
    side = math.isqrt(n // 2)
    nb = weight.shape[1]
    rows = nb // 2
    sds = jax.ShapeDtypeStruct
    scale = math.sqrt(n * V_CELLS / (n * nb * cells.shape[2]))

    def vm(*shape, dtype=F32):
        return pltpu.VMEM(shape, dtype)

    tall = TOPS * 16
    staged = pl.pallas_call(
        functools.partial(local_kernel, side),
        out_shape=(sds((4 * nb, LANE), F32), sds((rows, LANE), I32), sds((2, 2, side, side, 2, LANE), F32)),
        in_specs=[SMEM, SMEM, SMEM, VMEM, VMEM, VMEM],
        out_specs=(VMEM, VMEM, VMEM),
        scratch_shapes=[vm(4 * nb, LANE)] * 3 + [vm(nb, LANE, dtype=I32), vm(rows, LANE)],
        compiler_params=pltpu.CompilerParams(vmem_limit_bytes=LIMIT),
    )(seq, pairs, weight[0], vis.reshape(4 * nb, LANE), jones.reshape(-1, LANE), jnp.swapaxes(cells[0], 0, 1))
    sky, means = pl.pallas_call(
        functools.partial(whole_kernel, n, side, scale),
        out_shape=(sds((1, 4, LANE), F32), sds((4, 4, LANE), F32)),
        in_specs=[VMEM, VMEM, VMEM],
        out_specs=(VMEM, VMEM),
        scratch_shapes=[vm(2, side, side, 2, LANE)]
        + [vm(2, side, side, 2, LANE)] * 2
        + [vm(side, 2, side, 2, LANE)] * 2
        + [vm(2 * nb, LANE)]
        + [vm(side, side, 8, LANE)] * 2
        + [vm(side - 1, side, 8, LANE)] * 2
        + [vm(side, 8, LANE)] * 2
        + [vm(side - 1, 8, LANE)] * 2
        + [vm(tall, BOTS), vm(2, 8, LANE)]
        + [vm(tall, LANE * PER, dtype=BF16), vm(BOTS, LANE * PER, dtype=BF16)] * 2
        + [vm(2, side, side, 4, LANE), vm(side, side, 4, LANE)]
        + [vm(side, side, 2, LANE)] * 2
        + [vm(side - 1, side, 2, LANE)] * 2
        + [vm(side, 2, LANE)] * 2
        + [vm(side - 1, 2, LANE)] * 2
        + [pltpu.SemaphoreType.DMA((15,))] * 2,
        compiler_params=pltpu.CompilerParams(collective_id=0, has_side_effects=True, vmem_limit_bytes=LIMIT),
    )(*staged)
    return sky, means


def solution(mesh):
    both = ("grp", "bl")
    return jax.shard_map(
        functools.partial(per_device, mesh.shape["bl"]),
        mesh=mesh,
        in_specs=(P(both, None, None, None), P(both, None), P(both, None, None), P(), P("grp", None), P("grp")),
        out_specs=(P(both, None, None), P(both, None, None)),
        check_vma=False,
    )
```

time: 159 us -> 88.8 us (0.56)
  Pallas kernels: 0 us -> 85.4 us
  local copies, waits for them, and re-layouts: 35.3 us -> 2.53 us
  waiting for transfers between devices: 30.6 us -> 0 us
  starting transfers between devices: 27.6 us -> 0 us
  matrix products: 23.7 us -> 0 us
  blocking collectives: 20.9 us -> 0 us
  other arithmetic: 17.9 us -> 0 us
    pallas_call x0 -> x2, Pallas kernels: none -> 85.4 us  [the longest x1 69.2 us: per_device(): pl.pallas_call(functools.partial(whole_kernel, n, side, scale), out_shape...]
    all_to_all x1 -> x0, waiting for transfers between devices: 30.6 us -> none  [in_one_piece(): lax.all_to_all(both, axis, split_axis=split_dim, concat_axis=concat_dim,...]
    all_to_all x1 -> x0, starting transfers between devices: 27.6 us -> none  [in_one_piece(): lax.all_to_all(both, axis, split_axis=split_dim, concat_axis=concat_dim,...]
    dot_general x16 -> x0, matrix products: 23.7 us -> none  [add_rows(): lax.dot_general(placed, v_onehot, (((0,), (0,)), ((), ())), preferred_ele...]
    all_to_all x2 -> x0, blocking collectives: 20.9 us -> none  [the longest x1 16.5 us: sum_by_axis(): return jnp.sum(lax.all_to_all(own, far, 0, 0, tiled=True), axis=0)]
    dynamic_slice x16 -> x0, local copies, waits for them, and re-layouts: 13.6 us -> none  [per_device(): lax.scan(add_rows, start_rows, (value_blocks, index_blocks))]
    gather x8 -> x0, local copies, waits for them, and re-layouts: 11.6 us -> none  [the longest x1 3.49 us: per_device(): weight_sorted = jnp.take(sample_importance, pair_sequence, axis=1)]
    all_to_all x1 -> x0, other arithmetic: 4.64 us -> none  [in_one_piece(): lax.all_to_all(both, axis, split_axis=split_dim, concat_axis=concat_dim,...]
  transfers between devices with their start and end apart: 1 -> 0, of which waited for: 1 -> 0; matrix products, arithmetic and copies ran while one was open for 3% -> 0% of each run, Pallas kernels for 0% -> 0%
where the time goes in v2:
time: 88.8 us; the launch traced here: 88.6 us
  Pallas kernels  85.4 us (96%)
  local copies, waits for them, and re-layouts  2.53 us (3%)
    pallas_call x1, Pallas kernels, per_device(): pl.pallas_call(functools.partial(whole_kernel, n, side, scale), out_shape...  69.2 us
    pallas_call x1, Pallas kernels, per_device(): pl.pallas_call(functools.partial(local_kernel, side), out_shape=(sds((4 *...  16.2 us
    unnamed x4, local copies, waits for them, and re-layouts  2.53 us

profile of v2, /device:TPU:513, one launch (start us, length us, event | category | flops | bytes accessed | tf_op | source)
XLA Modules:
  0.0 88.6 jit_solution(17343211236401404067)
XLA Ops:
  0.6 16.2 %shard_map.77 = (f32[2048,128]{1,0:T(8,128)}, s32[256,128]{1,0:T(8,128)}, f32[2,2,8,8,2,128]{5,4,3,2,1,0:T(2,128)}) custom-call(s32[512]{0:T(512)} %seq.1, s32[2,512]{1,0:T(2,128)} %pairs.1, f32[512]{0:T(512)} %bitcast.9, f32[2048,128]{1,0:T(8,128)} %bitcast.6, f32[2048,128]{1,0:T(8,128)} %bitcast.7, s32[64,512]{1,0:T(8,128)} %bitcast.8), custom_call_target="tpu_custom_call" | custom-call | tf_op jit(solution)/shard_map/pallas_call | solution.py:348
  16.8 69.2 %shard_map.78 = (f32[1,4,128]{2,1,0:T(4,128)}, f32[4,4,128]{2,1,0:T(4,128)}) custom-call(f32[2048,128]{1,0:T(8,128)} %get-tuple-element.5.VAL, s32[256,128]{1,0:T(8,128)} %get-tuple-element.6.CR, f32[2,2,8,8,2,128]{5,4,3,2,1,0:T(2,128)} %get-tuple-element.7.XU), custom_call_target="tpu_custom_call" | custom-call | tf_op jit(solution)/shard_map/pallas_call | solution.py:356
  86.0 0.0 copy-start
  86.1 0.7 copy-done
  86.7 0.6 copy.10
  87.3 1.3 %copy.11 = f32[4,4,128]{2,1,0:T(4,128)} copy(f32[4,4,128]{2,1,0:T(4,128)} %get-tuple-element.11) | data formatting | bytes 16384
Async XLA Ops:
  86.0 0.7 copy-start

commit v3 on v2

v3 whole, which is shorter than its diff:
```python
import functools
import math

import jax
import jax.numpy as jnp
from jax import lax
from jax.experimental import pallas as pl
from jax.experimental.pallas import tpu as pltpu
from jax.sharding import PartitionSpec as P

MESH = pl.DeviceIdType.MESH
SMEM = pl.BlockSpec(memory_space=pltpu.SMEM)
HBM = pl.BlockSpec(memory_space=pltpu.HBM)
VMEM = pl.BlockSpec(memory_space=pltpu.VMEM)
F32 = jnp.float32
BF16 = jnp.bfloat16
I32 = jnp.int32
V_CELLS = 64
LANE = 128
TOPS = 32
BOTS = 256
PER = 16
EARLY = 5
MIB = 1024 * 1024
NT = (((1,), (1,)), ((), ()))


def half_pair(x0, x1, low):
    r0 = pltpu.roll(x0, 64, 1)
    r1 = pltpu.roll(x1, 64, 1)
    return jnp.where(low, x0, r1), jnp.where(low, r0, x1)


def interleave(x):
    row = lax.broadcasted_iota(I32, x.shape, 0)
    lane = lax.broadcasted_iota(I32, x.shape, 1)
    z = pltpu.roll(pltpu.roll(x, 4, 0), 64, 1)
    return jnp.where((row < 4) == (lane < 64), x, z)


def stage(side, seq, pairs, w, vis, jones, V, G, Q, CB, CR, CU, WR, WC):
    nb = seq.shape[0]
    low = lax.broadcasted_iota(I32, (1, LANE), 1) < 64

    def body(a, _):
        for core in range(2):
            for b in range(side):
                chip = side * a + b if core == 0 else a + side * b
                for j in range(2):
                    r = 2 * side * a + (nb // 4 * core + 2 * b + j)
                    slot = 8 * chip + (4 * core + 2 * j)
                    both = seq[slot], seq[slot + 1]
                    for h in range(2):
                        o = 8 * r + 4 * h
                        V[pl.ds(o, 4), :] = vis[pl.ds(4 * both[h], 4), :]
                        G[pl.ds(o, 4), :] = jones[pl.ds(4 * pairs[0, both[h]], 4), :]
                        Q[pl.ds(o, 4), :] = jones[pl.ds(4 * pairs[1, both[h]], 4), :]
                    cell = jnp.where(low, CB[pl.ds(both[0], 1), :], CB[pl.ds(both[1], 1), :])
                    CR[pl.ds(r, 1), :] = cell
                    CU[core, a, b, j:j + 1] = cell
                    WR[pl.ds(r, 1), :] = jnp.where(low, w[0, both[0]], w[0, both[1]])
        return 0

    lax.fori_loop(0, side, body, 0)
    for core in range(2):
        turned = jnp.transpose(WR[LANE * core:LANE * (core + 1), :])
        WC[core, 0:1] = turned[0:1]
        WC[core, 1:2] = turned[64:65]


def stage_stokes(V, G, Q, WR, VAL):
    low = lax.broadcasted_iota(I32, (8, LANE), 1) < 64

    def body(g, _):
        base = pl.multiple_of(64 * g, 64)

        def ld(ref, c):
            return half_pair(ref[pl.ds(base + c, 8, stride=8), :], ref[pl.ds(base + 4 + c, 8, stride=8), :], low)

        v = [ld(V, c) for c in range(4)]
        gp = [ld(G, c) for c in range(4)]
        gq = [ld(Q, c) for c in range(4)]
        W = []
        for o in range(2):
            for c in range(2):
                ar = ai = 0.0
                for m in range(2):
                    gr, gi = gp[2 * o + m]
                    dr, di = v[2 * m + c]
                    ar = ar + gr * dr - gi * di
                    ai = ai + gr * di + gi * dr
                W.append((ar, ai))
        C = []
        for o in range(2):
            for c in range(2):
                ar = ai = 0.0
                for m in range(2):
                    lr, li = W[2 * o + m]
                    gr, gi = gq[2 * c + m]
                    ar = ar + lr * gr + li * gi
                    ai = ai + li * gr - lr * gi
                C.append((ar, ai))
        wh = 0.5 * WR[pl.ds(pl.multiple_of(8 * g, 8), 8), :]
        comps = [
            C[0][0] + C[3][0],
            C[0][0] - C[3][0],
            C[1][0] + C[2][0],
            C[1][1] - C[2][1],
            C[0][1] + C[3][1],
            C[0][1] - C[3][1],
            C[1][1] + C[2][1],
            C[2][0] - C[1][0],
        ]
        for j, x in enumerate(comps):
            VAL[pl.ds(base + j, 8, stride=8), :] = wh * x
        return 0

    lax.fori_loop(0, VAL.shape[0] // 64, body, 0, unroll=4)


def build(first, val_of, cell_of, A, B):
    pos = lax.broadcasted_iota(I32, (16, LANE), 0).astype(F32).astype(BF16)
    zero = jnp.zeros((16, LANE), BF16)
    one = jnp.ones((16, LANE), BF16)
    for q in range(PER):
        s = slice(LANE * q, LANE * (q + 1))
        val = val_of(first + q)
        hi = val.astype(BF16)
        lo = (val - hi.astype(F32)).astype(BF16)
        both = jnp.concatenate([hi, lo], 0)
        cell = cell_of(first + q)
        top = jnp.broadcast_to((cell >> 8).astype(F32), (16, LANE)).astype(BF16)
        rel = jnp.broadcast_to((cell & 255).astype(F32), (16, LANE)).astype(BF16) - pos
        for i in range(TOPS):
            A[16 * i:16 * i + 16, s] = jnp.where(top == BF16(i), both, zero)
        for i in range(BOTS // 16):
            B[16 * i:16 * i + 16, s] = jnp.where(rel == BF16(16 * i), one, zero)


def add_rows(first, rows, val_of, cell_of, A, B, ACC):
    def dot(p):
        ACC[...] += lax.dot_general(A[p][...], B[p][...], NT, preferred_element_type=F32)

    def step(s, _):
        base = first + 2 * PER * s
        build(base + PER, val_of, cell_of, A[1], B[1])
        dot(0)
        build(base + 2 * PER, val_of, cell_of, A[0], B[0])
        dot(1)
        return 0

    lax.fori_loop(0, rows // (2 * PER), step, 0)


def remote(src, dst, send, recv, i, d):
    return pltpu.make_async_remote_copy(
        src_ref=src,
        dst_ref=dst,
        send_sem=send.at[i],
        recv_sem=recv.at[i],
        device_id={"bl": d},
        device_id_type=MESH,
    )


def local_kernel(side, *refs):
    outside, (VAL, CR, CU, WC), inside, (V, G, Q, CB, WR, sem) = refs[:6], refs[6:10], refs[10:16], refs[16:]
    copies = [pltpu.make_async_copy(a, b, sem.at[i]) for i, (a, b) in enumerate(zip(outside, inside))]
    for copy in copies:
        copy.start()
    seq, pairs, w, vis, jones, cells_t = inside
    copies[5].wait()
    for j in range(cells_t.shape[1] // LANE):
        blk = cells_t[:, LANE * j:LANE * (j + 1)]
        CB[LANE * j:LANE * (j + 1), :] = jnp.transpose(jnp.concatenate([blk, blk], 0))
    for copy in copies[:5]:
        copy.wait()
    stage(side, seq, pairs, w, vis, jones, V, G, Q, CB, CR, CU, WR, WC)
    stage_stokes(V, G, Q, WR, VAL)


def spread(row):
    return jnp.broadcast_to(row.astype(F32), (16, LANE)).astype(BF16)


def weigh_cells(CT, W4, HS, HB):
    pos = lax.broadcasted_iota(I32, (16, LANE), 0).astype(F32).astype(BF16)
    zero = jnp.zeros((16, LANE), BF16)
    one = jnp.ones((16, LANE), BF16)
    high = HB.shape[0]
    pitch = high + 8

    def body(g, _):
        wrow = W4[pl.ds(g // 4, 1), :]
        whi = wrow.astype(BF16)
        wlo = spread(wrow - whi.astype(F32))
        whi = spread(whi)
        for q in range(16):
            cell = CT[pl.ds(16 * g + q, 1), :]
            up = spread(cell >> 7) - pos
            along = spread(cell & 127) - pos
            hits = [up == BF16(16 * i) for i in range(high // 16)]
            left = jnp.concatenate([jnp.where(m, whi, zero) for m in hits] + [jnp.where(m, wlo, zero) for m in hits], 0)
            right = jnp.concatenate([jnp.where(along == BF16(16 * i), one, zero) for i in range(8)], 0)
            both = lax.dot_general(left, right, NT, preferred_element_type=F32)
            HS[pitch * q:pitch * q + high, :] = both[:high] + both[high:]
        for u in range(high):
            x = jnp.concatenate([HS[pl.ds(u, 8, stride=pitch), :], HS[pl.ds(u + 8 * pitch, 8, stride=pitch), :]], 0)
            hi = x.astype(BF16)
            HB[u, pl.ds(16 * g, 16), 0:LANE] = hi
            HB[u, pl.ds(16 * g, 16), LANE:2 * LANE] = (x - hi.astype(F32)).astype(BF16)
        return 0

    lax.fori_loop(0, CT.shape[0] // 16, body, 0)


def whole_kernel(n, side, scale, VAL, CR, CU, WC, sky, means, PC, PW, X, XW, Y, YW, R1, RA, T, U,
                 ACC, A0, B0, A1, B1, CT, WT, W4, HS, HB, GR, PG, HA, K, L, send, recv):
    me = lax.axis_index("bl")
    core = lax.rem(me, 2)
    chip = me // 2
    x = chip // side
    y = lax.rem(chip, side)
    mate = 2 * chip + 1 - core
    first = x + core * (y - x)
    second = y + core * (x - y)
    step1 = 2 * side + core * (2 - 2 * side)
    step2 = 2 + core * (2 * side - 2)
    rows = CR.shape[0]

    def on_first(k):
        place = lax.rem(first + k, side)
        return place, me + (place - first) * step1

    def on_second(k):
        place = lax.rem(second + k, side)
        return place, me + (place - second) * step2

    def landed(ref, i):
        remote(ref, ref, send, recv, i, mate).wait_recv()

    def sent(ref, i):
        remote(ref, ref, send, recv, i, mate).wait_send()

    barrier = pltpu.get_barrier_semaphore()
    for k in range(1, side):
        for d in (on_first(k)[1], on_second(k)[1]):
            pl.semaphore_signal(barrier, inc=1, device_id={"bl": d}, device_id_type=MESH)
    pl.semaphore_signal(barrier, inc=1, device_id={"bl": mate}, device_id_type=MESH)
    pl.semaphore_wait(barrier, 2 * side - 1)

    remote(CU.at[1 - core], PC, send, recv, 0, mate).start()
    remote(WC.at[1 - core], PW, send, recv, 3, mate).start()
    remote(VAL.at[1 - core], R1, send, recv, 6, mate).start()

    def own_val(r):
        r = lax.rem(r, rows)
        unit = r // 2
        half = rows // 4
        at = pl.multiple_of(8 * lax.rem(r, 2), 8)
        return VAL[unit // half, lax.rem(unit, half) // side, lax.rem(unit, side), pl.ds(at, 8), :]

    def own_cell(r):
        return CR[pl.ds(lax.rem(r, rows), 1), :]

    bufs = (A0, A1), (B0, B1)
    ACC[...] = jnp.zeros_like(ACC)
    build(0, own_val, own_cell, A0, B0)
    landed(PC, 0)
    landed(PW, 3)
    landed(R1, 6)

    def fold(i, _):
        R1[i] = R1[i] + VAL[core, i]
        return 0

    lax.fori_loop(0, side, fold, 0)
    for k in range(1, side):
        place, d = on_first(k)
        remote(R1.at[place], RA.at[k - 1], send, recv, 7, d).start()
    for k in range(1, side):
        place, d = on_first(k)
        remote(CU.at[core, place], X.at[0, k], send, recv, 1, d).start()
        remote(PC.at[place], X.at[1, k], send, recv, 1, d).start()
        remote(WC.at[core], XW.at[0, k], send, recv, 4, d).start()
        remote(PW, XW.at[1, k], send, recv, 4, d).start()
    X[0, 0] = CU[core, first]
    X[1, 0] = PC[first]
    XW[0, 0] = WC[core]
    XW[1, 0] = PW[...]
    add_rows(0, EARLY * rows // 8, own_val, own_cell, *bufs, ACC)
    landed(RA, 7)
    for i in range(side):
        t = R1[first, i]
        for k in range(side - 1):
            t = t + RA[k, i]
        T[i] = t
    for k in range(1, side):
        place, d = on_second(k)
        remote(T.at[place], U.at[k - 1], send, recv, 8, d).start()
    landed(X.at[:, 1:side], 1)
    landed(XW.at[:, 1:side], 4)
    for k in range(1, side):
        place, d = on_second(k)
        remote(X.at[:, :, place], Y.at[k], send, recv, 2, d).start()
        remote(XW, YW.at[k], send, recv, 5, d).start()
    Y[0] = X[:, :, second]
    YW[0] = XW[...]
    add_rows(EARLY * rows // 8, (8 - EARLY) * rows // 8, own_val, own_cell, *bufs, ACC)
    landed(Y.at[1:side], 2)
    landed(YW.at[1:side], 5)
    for j in range(2):
        CT[LANE * j:LANE * (j + 1), :] = jnp.transpose(Y[:, :, :, j, :].reshape(n, LANE))
    for h in range(2):
        WT[...] = jnp.transpose(YW[:, :, :, h, :].reshape(n, LANE))
        for j in range(2):
            W4[2 * j + h:2 * j + h + 1, :] = WT[pl.ds(2 * side * first + 2 * second + j, 1), :]
    weigh_cells(CT, W4, HS, HB)
    landed(U, 8)

    total = T[second] + jnp.sum(U[...], axis=0)
    low = lax.broadcasted_iota(I32, (1, LANE), 1) < 64
    weights = jnp.sum(W4[...], axis=1, keepdims=True)
    averages = []
    for j in range(2):
        m = total[8 * j:8 * j + 8] / jnp.where(low, weights[2 * j:2 * j + 1], weights[2 * j + 1:2 * j + 2])
        averages.append(m)
        z = interleave(m)
        means[2 * j] = z[0:4]
        means[2 * j + 1] = z[4:8]
    m = jnp.concatenate(averages, 1)
    hi = m.astype(BF16)
    lo = (m - hi.astype(F32)).astype(BF16)
    left = jnp.concatenate([hi, lo], 0)
    for u in range(HB.shape[0]):
        both = jnp.dot(left, HB[u], preferred_element_type=F32)
        both = both[0:8] + both[8:16]
        i, h = u // 2, u % 2
        s = slice(LANE * h, LANE * (h + 1))
        z = ACC[16 * i:16 * i + 8, s] + ACC[16 * i + 8:16 * i + 16, s] - (both[:, :LANE] + both[:, LANE:])
        z = interleave(z) * scale
        for e in range(2):
            d = 2 * u + e
            at = (d // 2 // side, d // 2 % side) if e == 0 else (d // 2 % side, d // 2 // side)
            GR[e, at[0], at[1]] = z[4 * e:4 * e + 4]

    remote(GR.at[1 - core], PG, send, recv, 9, mate).start()
    landed(PG, 9)
    PG[...] = PG[...] + GR[core]
    for k in range(1, side):
        place, d = on_first(k)
        remote(PG.at[place], HA.at[k - 1], send, recv, 10, d).start()
    landed(HA, 10)
    K[...] = PG[first] + jnp.sum(HA[...], axis=0)
    for k in range(1, side):
        place, d = on_second(k)
        remote(K.at[place], L.at[k - 1], send, recv, 11, d).start()
    landed(L, 11)
    sky[0] = K[second] + jnp.sum(L[...], axis=0)
    for ref, i in (
        (PC, 0), (X.at[:, 1:side], 1), (Y.at[1:side], 2), (PW, 3), (XW.at[:, 1:side], 4), (YW.at[1:side], 5),
        (R1, 6), (RA, 7), (U, 8), (PG, 9), (HA, 10), (L, 11),
    ):
        sent(ref, i)


def per_device(n, vis, weight, cells, jones, pairs, seq):
    side = math.isqrt(n // 2)
    nb = weight.shape[1]
    rows = nb // 2
    sds = jax.ShapeDtypeStruct
    scale = math.sqrt(n * V_CELLS / (n * nb * cells.shape[2]))

    def vm(*shape, dtype=F32):
        return pltpu.VMEM(shape, dtype)

    tall = TOPS * 16
    val, *staged = pl.pallas_call(
        functools.partial(local_kernel, side),
        out_shape=(
            sds((4 * nb, LANE), F32),
            sds((rows, LANE), I32),
            sds((2, side, side, 2, LANE), I32),
            sds((2, 2, LANE), F32),
        ),
        in_specs=[HBM] * 6,
        out_specs=(VMEM,) * 4,
        scratch_shapes=[pltpu.SMEM((nb,), I32), pltpu.SMEM((2, nb), I32), pltpu.SMEM((1, nb), F32)]
        + [vm(4 * nb, LANE), vm(4 * jones.shape[0], LANE), vm(cells.shape[2], nb, dtype=I32)]
        + [vm(4 * nb, LANE)] * 3
        + [vm(nb, LANE, dtype=I32), vm(rows, LANE), pltpu.SemaphoreType.DMA((6,))],
        compiler_params=pltpu.CompilerParams(vmem_limit_bytes=12 * MIB),
    )(seq, pairs, weight, vis.reshape(4 * nb, LANE), jones.reshape(-1, LANE), jnp.swapaxes(cells[0], 0, 1))
    sky, means = pl.pallas_call(
        functools.partial(whole_kernel, n, side, scale),
        out_shape=(sds((1, 4, LANE), F32), sds((4, 4, LANE), F32)),
        in_specs=[VMEM] * 4,
        out_specs=(VMEM, VMEM),
        scratch_shapes=[vm(side, side, 2, LANE, dtype=I32), vm(2, LANE)]
        + [vm(2, side, side, 2, LANE, dtype=I32), vm(2, side, 2, LANE)]
        + [vm(side, 2, side, 2, LANE, dtype=I32), vm(side, 2, side, 2, LANE)]
        + [vm(side, side, 16, LANE), vm(side - 1, side, 16, LANE), vm(side, 16, LANE), vm(side - 1, 16, LANE)]
        + [vm(tall, BOTS)]
        + [vm(tall, LANE * PER, dtype=BF16), vm(BOTS, LANE * PER, dtype=BF16)] * 2
        + [vm(rows, LANE, dtype=I32), vm(n, LANE), vm(4, LANE)]
        + [vm(16 * (n // 2 + 8), LANE), vm(n // 2, rows, 2 * LANE, dtype=BF16)]
        + [vm(2, side, side, 4, LANE), vm(side, side, 4, LANE), vm(side - 1, side, 4, LANE)]
        + [vm(side, 4, LANE), vm(side - 1, 4, LANE)]
        + [pltpu.SemaphoreType.DMA((12,))] * 2,
        compiler_params=pltpu.CompilerParams(collective_id=0, has_side_effects=True, vmem_limit_bytes=32 * MIB),
    )(val.reshape(2, side, side, 16, LANE), *staged)
    return sky, means


def solution(mesh):
    both = ("grp", "bl")
    return jax.shard_map(
        functools.partial(per_device, mesh.shape["bl"]),
        mesh=mesh,
        in_specs=(P(both, None, None, None), P(both, None), P(both, None, None), P(), P("grp", None), P("grp")),
        out_specs=(P(both, None, None), P(both, None, None)),
        check_vma=False,
    )
```

time: 88.8 us -> 74.4 us (0.84)
  Pallas kernels: 85.4 us -> 66.9 us
  local copies, waits for them, and re-layouts: 2.53 us -> 6.57 us
    pallas_call x1, Pallas kernels: 16.2 us -> 4.87 us  [per_device(): pl.pallas_call(functools.partial(local_kernel, side), out_shape=(sds((4 *...]
    pallas_call x1, Pallas kernels: 69.2 us -> 62 us  [per_device(): pl.pallas_call(functools.partial(whole_kernel, n, side, scale), out_shape...]
    unnamed x4 -> x14, local copies, waits for them, and re-layouts: 2.53 us -> 6.57 us
where the time goes in v3:
time: 74.4 us; the launch traced here: 74.1 us
  Pallas kernels  66.9 us (90%)
  local copies, waits for them, and re-layouts  6.57 us (9%)
    pallas_call x1, Pallas kernels, per_device(): pl.pallas_call(functools.partial(whole_kernel, n, side, scale), out_shape...  62 us
    unnamed x14, local copies, waits for them, and re-layouts  6.57 us
    pallas_call x1, Pallas kernels, per_device(): pl.pallas_call(functools.partial(local_kernel, side), out_shape=(sds((4 *...  4.87 us

profile of v3, /device:TPU:513, one launch (start us, length us, event | category | flops | bytes accessed | tf_op | source)
XLA Modules:
  0.0 74.1 jit_solution(8671561721399928466)
XLA Ops:
  0.6 0.0 copy-start.3
  0.6 0.7 copy-done.3
  1.3 0.0 copy-start
  1.3 1.2 %copy-done = f32[1,512,4,128]{3,2,1,0:T(4,128)S(1)} copy-done((f32[1,512,4,128]{3,2,1,0:T(4,128)S(1)}, f32[1,512,4,128]{3,2,1,0:T(4,128)}, u32[]{:S(2)}) %copy-start) | copy-done | bytes 1048600
  2.5 0.0 copy-start.1
  2.5 1.2 %copy-done.1 = f32[512,4,128]{2,1,0:T(4,128)S(1)} copy-done((f32[512,4,128]{2,1,0:T(4,128)S(1)}, f32[512,4,128]{2,1,0:T(4,128)}, u32[]{:S(2)}) %copy-start.1) | copy-done | bytes 1048600
  3.8 0.0 copy-start.2
  3.8 0.9 %copy-done.2 = s32[1,512,64]{1,2,0:T(8,128)S(1)} copy-done((s32[1,512,64]{1,2,0:T(8,128)S(1)}, s32[1,512,64]{1,2,0:T(8,128)}, u32[]{:S(2)}) %copy-start.2) | copy-done | bytes 131096
  4.7 0.0 copy-start.4
  4.7 0.7 copy-done.4
  5.4 0.0 copy-start.5
  5.4 0.7 copy-done.5
  6.0 4.9 %shard_map.77 = (f32[2048,128]{1,0:T(8,128)S(1)}, s32[256,128]{1,0:T(8,128)S(1)}, s32[2,8,8,2,128]{4,3,2,1,0:T(2,128)S(1)}, f32[2,2,128]{2,1,0:T(2,128)S(1)}) custom-call(s32[512]{0:T(512)S(1)} %copy-done.4, s32[2,512]{1,0:T(2,128)S(1)} %copy-done.3, f32[1,512]{1,0:T(1,128)S(1)} %copy-done.5, f32[2048,128]{1,0:T(8,128)S(1)} %bitcast.7, ...), custom_call_target="tpu_custom_call" | custom-call | tf_op jit(solution)/shard_map/pallas_call | solution.py:378
  10.9 62.0 %shard_map.78 = (f32[1,4,128]{2,1,0:T(4,128)S(1)}, f32[4,4,128]{2,1,0:T(4,128)S(1)}) custom-call(f32[2,8,8,16,128]{4,3,2,1,0:T(8,128)S(1)} %bitcast.6, s32[256,128]{1,0:T(8,128)S(1)} %get-tuple-element.7.CR, s32[2,8,8,2,128]{4,3,2,1,0:T(2,128)S(1)} %get-tuple-element.8.CU, f32[2,2,128]{2,1,0:T(2,128)S(1)} %get-tuple-element.9.WC), custom_call_target="tpu_custom_call" | custom-call | tf_op jit(solution)/shard_map/pallas_call | solution.py:394
  72.9 0.6 copy.10
  73.5 0.6 copy.11
Async XLA Ops:
  0.6 0.7 copy-start.3
  1.3 1.2 %copy-start = (f32[1,512,4,128]{3,2,1,0:T(4,128)S(1)}, f32[1,512,4,128]{3,2,1,0:T(4,128)}, u32[]{:S(2)}) copy-start(f32[1,512,4,128]{3,2,1,0:T(4,128)} %param.6) | copy-start | bytes 3145732
  2.5 1.2 %copy-start.1 = (f32[512,4,128]{2,1,0:T(4,128)S(1)}, f32[512,4,128]{2,1,0:T(4,128)}, u32[]{:S(2)}) copy-start(f32[512,4,128]{2,1,0:T(4,128)} %param.9) | copy-start | bytes 3145732
  3.8 0.9 %copy-start.2 = (s32[1,512,64]{1,2,0:T(8,128)S(1)}, s32[1,512,64]{1,2,0:T(8,128)}, u32[]{:S(2)}) copy-start(s32[1,512,64]{1,2,0:T(8,128)} %param.8) | copy-start | bytes 393220
  4.7 0.7 copy-start.4
  5.4 0.7 copy-start.5

commit v4 on v3

--- a/solution.py
+++ b/solution.py
@@ -10,7 +10,6 @@
 
 MESH = pl.DeviceIdType.MESH
 SMEM = pl.BlockSpec(memory_space=pltpu.SMEM)
-HBM = pl.BlockSpec(memory_space=pltpu.HBM)
 VMEM = pl.BlockSpec(memory_space=pltpu.VMEM)
 F32 = jnp.float32
 BF16 = jnp.bfloat16
@@ -20,7 +19,6 @@
 TOPS = 32
 BOTS = 256
 PER = 16
-EARLY = 5
 MIB = 1024 * 1024
 NT = (((1,), (1,)), ((), ()))
 
@@ -68,7 +66,7 @@
         WC[core, 1:2] = turned[64:65]
 
 
-def stage_stokes(V, G, Q, WR, VAL):
+def stage_stokes(V, G, Q, WR, WQ, VAL):
     low = lax.broadcasted_iota(I32, (8, LANE), 1) < 64
 
     def body(g, _):
@@ -100,7 +98,10 @@
                     ar = ar + lr * gr + li * gi
                     ai = ai + li * gr - lr * gi
                 C.append((ar, ai))
-        wh = 0.5 * WR[pl.ds(pl.multiple_of(8 * g, 8), 8), :]
+        eight = pl.ds(pl.multiple_of(8 * g, 8), 8)
+        weight = WR[eight, :]
+        WQ[eight, :] = weight.astype(BF16).astype(F32) / weight
+        wh = 0.5 * weight
         comps = [
             C[0][0] + C[3][0],
             C[0][0] - C[3][0],
@@ -163,20 +164,12 @@
     )
 
 
-def local_kernel(side, *refs):
-    outside, (VAL, CR, CU, WC), inside, (V, G, Q, CB, WR, sem) = refs[:6], refs[6:10], refs[10:16], refs[16:]
-    copies = [pltpu.make_async_copy(a, b, sem.at[i]) for i, (a, b) in enumerate(zip(outside, inside))]
-    for copy in copies:
-        copy.start()
-    seq, pairs, w, vis, jones, cells_t = inside
-    copies[5].wait()
+def local_kernel(side, seq, pairs, w, vis, jones, cells_t, VAL, CR, CU, WC, WQ, V, G, Q, CB, WR):
     for j in range(cells_t.shape[1] // LANE):
         blk = cells_t[:, LANE * j:LANE * (j + 1)]
         CB[LANE * j:LANE * (j + 1), :] = jnp.transpose(jnp.concatenate([blk, blk], 0))
-    for copy in copies[:5]:
-        copy.wait()
     stage(side, seq, pairs, w, vis, jones, V, G, Q, CB, CR, CU, WR, WC)
-    stage_stokes(V, G, Q, WR, VAL)
+    stage_stokes(V, G, Q, WR, WQ, VAL)
 
 
 def spread(row):
@@ -191,19 +184,14 @@
     pitch = high + 8
 
     def body(g, _):
-        wrow = W4[pl.ds(g // 4, 1), :]
-        whi = wrow.astype(BF16)
-        wlo = spread(wrow - whi.astype(F32))
-        whi = spread(whi)
+        weight = spread(W4[pl.ds(g // 4, 1), :])
         for q in range(16):
             cell = CT[pl.ds(16 * g + q, 1), :]
             up = spread(cell >> 7) - pos
             along = spread(cell & 127) - pos
-            hits = [up == BF16(16 * i) for i in range(high // 16)]
-            left = jnp.concatenate([jnp.where(m, whi, zero) for m in hits] + [jnp.where(m, wlo, zero) for m in hits], 0)
+            left = jnp.concatenate([jnp.where(up == BF16(16 * i), weight, zero) for i in range(high // 16)], 0)
             right = jnp.concatenate([jnp.where(along == BF16(16 * i), one, zero) for i in range(8)], 0)
-            both = lax.dot_general(left, right, NT, preferred_element_type=F32)
-            HS[pitch * q:pitch * q + high, :] = both[:high] + both[high:]
+            HS[pitch * q:pitch * q + high, :] = lax.dot_general(left, right, NT, preferred_element_type=F32)
         for u in range(high):
             x = jnp.concatenate([HS[pl.ds(u, 8, stride=pitch), :], HS[pl.ds(u + 8 * pitch, 8, stride=pitch), :]], 0)
             hi = x.astype(BF16)
@@ -214,7 +202,7 @@
     lax.fori_loop(0, CT.shape[0] // 16, body, 0)
 
 
-def whole_kernel(n, side, scale, VAL, CR, CU, WC, sky, means, PC, PW, X, XW, Y, YW, R1, RA, T, U,
+def whole_kernel(n, side, scale, VAL, CR, CU, WC, WQ, sky, means, PC, PW, X, XW, Y, YW, R1, RA, T, U,
                  ACC, A0, B0, A1, B1, CT, WT, W4, HS, HB, GR, PG, HA, K, L, send, recv):
     me = lax.axis_index("bl")
     core = lax.rem(me, 2)
@@ -258,7 +246,7 @@
         unit = r // 2
         half = rows // 4
         at = pl.multiple_of(8 * lax.rem(r, 2), 8)
-        return VAL[unit // half, lax.rem(unit, half) // side, lax.rem(unit, side), pl.ds(at, 8), :]
+        return VAL[unit // half, lax.rem(unit, half) // side, lax.rem(unit, side), pl.ds(at, 8), :] * WQ[pl.ds(r, 1), :]
 
     def own_cell(r):
         return CR[pl.ds(lax.rem(r, rows), 1), :]
@@ -268,16 +256,6 @@
     build(0, own_val, own_cell, A0, B0)
     landed(PC, 0)
     landed(PW, 3)
-    landed(R1, 6)
-
-    def fold(i, _):
-        R1[i] = R1[i] + VAL[core, i]
-        return 0
-
-    lax.fori_loop(0, side, fold, 0)
-    for k in range(1, side):
-        place, d = on_first(k)
-        remote(R1.at[place], RA.at[k - 1], send, recv, 7, d).start()
     for k in range(1, side):
         place, d = on_first(k)
         remote(CU.at[core, place], X.at[0, k], send, recv, 1, d).start()
@@ -288,7 +266,26 @@
     X[1, 0] = PC[first]
     XW[0, 0] = WC[core]
     XW[1, 0] = PW[...]
-    add_rows(0, EARLY * rows // 8, own_val, own_cell, *bufs, ACC)
+    landed(R1, 6)
+
+    def fold(i, _):
+        R1[i] = R1[i] + VAL[core, i]
+        return 0
+
+    lax.fori_loop(0, side, fold, 0)
+    for k in range(1, side):
+        place, d = on_first(k)
+        remote(R1.at[place], RA.at[k - 1], send, recv, 7, d).start()
+    add_rows(0 * rows // 8, 4 * rows // 8, own_val, own_cell, *bufs, ACC)
+    landed(X.at[:, 1:side], 1)
+    landed(XW.at[:, 1:side], 4)
+    for k in range(1, side):
+        place, d = on_second(k)
+        remote(X.at[:, :, place], Y.at[k], send, recv, 2, d).start()
+        remote(XW, YW.at[k], send, recv, 5, d).start()
+    Y[0] = X[:, :, second]
+    YW[0] = XW[...]
+    add_rows(4 * rows // 8, 1 * rows // 8, own_val, own_cell, *bufs, ACC)
     landed(RA, 7)
     for i in range(side):
         t = R1[first, i]
@@ -298,15 +295,7 @@
     for k in range(1, side):
         place, d = on_second(k)
         remote(T.at[place], U.at[k - 1], send, recv, 8, d).start()
-    landed(X.at[:, 1:side], 1)
-    landed(XW.at[:, 1:side], 4)
-    for k in range(1, side):
-        place, d = on_second(k)
-        remote(X.at[:, :, place], Y.at[k], send, recv, 2, d).start()
-        remote(XW, YW.at[k], send, recv, 5, d).start()
-    Y[0] = X[:, :, second]
-    YW[0] = XW[...]
-    add_rows(EARLY * rows // 8, (8 - EARLY) * rows // 8, own_val, own_cell, *bufs, ACC)
+    add_rows(5 * rows // 8, 3 * rows // 8, own_val, own_cell, *bufs, ACC)
     landed(Y.at[1:side], 2)
     landed(YW.at[1:side], 5)
     for j in range(2):
@@ -382,19 +371,17 @@
             sds((rows, LANE), I32),
             sds((2, side, side, 2, LANE), I32),
             sds((2, 2, LANE), F32),
+            sds((rows, LANE), F32),
         ),
-        in_specs=[HBM] * 6,
-        out_specs=(VMEM,) * 4,
-        scratch_shapes=[pltpu.SMEM((nb,), I32), pltpu.SMEM((2, nb), I32), pltpu.SMEM((1, nb), F32)]
-        + [vm(4 * nb, LANE), vm(4 * jones.shape[0], LANE), vm(cells.shape[2], nb, dtype=I32)]
-        + [vm(4 * nb, LANE)] * 3
-        + [vm(nb, LANE, dtype=I32), vm(rows, LANE), pltpu.SemaphoreType.DMA((6,))],
+        in_specs=[SMEM] * 3 + [VMEM] * 3,
+        out_specs=(VMEM,) * 5,
+        scratch_shapes=[vm(4 * nb, LANE)] * 3 + [vm(nb, LANE, dtype=I32), vm(rows, LANE)],
         compiler_params=pltpu.CompilerParams(vmem_limit_bytes=12 * MIB),
     )(seq, pairs, weight, vis.reshape(4 * nb, LANE), jones.reshape(-1, LANE), jnp.swapaxes(cells[0], 0, 1))
     sky, means = pl.pallas_call(
         functools.partial(whole_kernel, n, side, scale),
         out_shape=(sds((1, 4, LANE), F32), sds((4, 4, LANE), F32)),
-        in_specs=[VMEM] * 4,
+        in_specs=[VMEM] * 5,
         out_specs=(VMEM, VMEM),
         scratch_shapes=[vm(side, side, 2, LANE, dtype=I32), vm(2, LANE)]
         + [vm(2, side, side, 2, LANE, dtype=I32), vm(2, side, 2, LANE)]

time: 74.4 us -> 71.1 us (0.956)
  Pallas kernels: 66.9 us -> 63.6 us
    pallas_call x1, Pallas kernels: 62 us -> 58.6 us  [per_device(): pl.pallas_call(functools.partial(whole_kernel, n, side, scale), out_shape...]
where the time goes in v4:
time: 71.1 us; the launch traced here: 70.8 us
  Pallas kernels  63.6 us (89%)
  local copies, waits for them, and re-layouts  6.57 us (9%)
    pallas_call x1, Pallas kernels, per_device(): pl.pallas_call(functools.partial(whole_kernel, n, side, scale), out_shape...  58.6 us
    unnamed x14, local copies, waits for them, and re-layouts  6.57 us
    pallas_call x1, Pallas kernels, per_device(): pl.pallas_call(functools.partial(local_kernel, side), out_shape=(sds((4 *...  5.03 us

profile of v4, /device:TPU:513, one launch (start us, length us, event | category | flops | bytes accessed | tf_op | source)
XLA Modules:
  0.0 70.8 jit_solution(3960709059128129288)
XLA Ops:
  0.6 0.0 copy-start.3
  0.6 0.7 copy-done.3
  1.3 0.0 copy-start
  1.3 1.2 %copy-done = f32[1,512,4,128]{3,2,1,0:T(4,128)S(1)} copy-done((f32[1,512,4,128]{3,2,1,0:T(4,128)S(1)}, f32[1,512,4,128]{3,2,1,0:T(4,128)}, u32[]{:S(2)}) %copy-start) | copy-done | bytes 1048600
  2.5 0.0 copy-start.1
  2.5 1.2 %copy-done.1 = f32[512,4,128]{2,1,0:T(4,128)S(1)} copy-done((f32[512,4,128]{2,1,0:T(4,128)S(1)}, f32[512,4,128]{2,1,0:T(4,128)}, u32[]{:S(2)}) %copy-start.1) | copy-done | bytes 1048600
  3.8 0.0 copy-start.2
  3.8 0.9 %copy-done.2 = s32[1,512,64]{1,2,0:T(8,128)S(1)} copy-done((s32[1,512,64]{1,2,0:T(8,128)S(1)}, s32[1,512,64]{1,2,0:T(8,128)}, u32[]{:S(2)}) %copy-start.2) | copy-done | bytes 131096
  4.7 0.0 copy-start.4
  4.7 0.7 copy-done.4
  5.4 0.0 copy-start.5
  5.4 0.7 copy-done.5
  6.0 5.0 %shard_map.77 = (f32[2048,128]{1,0:T(8,128)S(1)}, s32[256,128]{1,0:T(8,128)S(1)}, s32[2,8,8,2,128]{4,3,2,1,0:T(2,128)S(1)}, f32[2,2,128]{2,1,0:T(2,128)S(1)}, f32[256,128]{1,0:T(8,128)S(1)}) custom-call(s32[512]{0:T(512)S(1)} %copy-done.4, s32[2,512]{1,0:T(2,128)S(1)} %copy-done.3, f32[1,512]{1,0:T(1,128)S(1)} %copy-done.5, f32[2048,128]{1,0:T(8,128)S(1)} %bitcast.6, ...), custom_call_target="tpu_custom_call" | custom-call | tf_op jit(solution)/shard_map/pallas_call | solution.py:367
  11.1 58.6 %shard_map.78 = (f32[1,4,128]{2,1,0:T(4,128)S(1)}, f32[4,4,128]{2,1,0:T(4,128)S(1)}) custom-call(f32[2,8,8,16,128]{4,3,2,1,0:T(8,128)S(1)} %bitcast.8, s32[256,128]{1,0:T(8,128)S(1)} %get-tuple-element.8.CR, s32[2,8,8,2,128]{4,3,2,1,0:T(2,128)S(1)} %get-tuple-element.9.CU, f32[2,2,128]{2,1,0:T(2,128)S(1)} %get-tuple-element.10.WC, ...), custom_call_target="tpu_custom_call" | custom-call | tf_op jit(solution)/shard_map/pallas_call | solution.py:381
  69.6 0.6 copy.10
  70.2 0.6 copy.11
Async XLA Ops:
  0.6 0.7 copy-start.3
  1.3 1.2 %copy-start = (f32[1,512,4,128]{3,2,1,0:T(4,128)S(1)}, f32[1,512,4,128]{3,2,1,0:T(4,128)}, u32[]{:S(2)}) copy-start(f32[1,512,4,128]{3,2,1,0:T(4,128)} %param.6) | copy-start | bytes 3145732
  2.5 1.2 %copy-start.1 = (f32[512,4,128]{2,1,0:T(4,128)S(1)}, f32[512,4,128]{2,1,0:T(4,128)}, u32[]{:S(2)}) copy-start(f32[512,4,128]{2,1,0:T(4,128)} %param.9) | copy-start | bytes 3145732
  3.8 0.9 %copy-start.2 = (s32[1,512,64]{1,2,0:T(8,128)S(1)}, s32[1,512,64]{1,2,0:T(8,128)}, u32[]{:S(2)}) copy-start(s32[1,512,64]{1,2,0:T(8,128)} %param.8) | copy-start | bytes 393220
  4.7 0.7 copy-start.4
  5.4 0.7 copy-start.5
